TPU v7x, 512 devices: a 8x2x16 block of a 8x8x16 slice. The times are simulated.
512 devices in a mesh: groups: 2 (over y), rows: 16 (over z), cols: 8 (over x), depth: 2 (over core).
Axes of the slice: x: 8, y: 2, z: 16, core: 2. Of those that a mesh axis runs over, the one named last changes fastest.
The devices are a block of a 8x8x16 slice.
Arguments:
- tensor: float32 [512, 128, 256], P(('groups', 'rows'), 'cols', 'depth'), parts along dimension 0, may hold values from -6 to 6
- start_one: float32 [512, 64], P(('groups', 'rows')), parts along dimension 0, may hold values from -0.375 to 0.375
- start_two: float32 [256, 64], P(('groups', 'cols')), parts along dimension 0, may hold values from -0.5 to 0.5
- start_three: float32 [512, 32], P(('groups', 'depth')), parts along dimension 0, may hold values from -0.375 to 0.375
Outputs:
- final_one: float32 [512, 64], P(('groups', 'rows')), parts along dimension 0
- final_two: float32 [256, 64], P(('groups', 'cols')), parts along dimension 0
- final_three: float32 [512, 32], P(('groups', 'depth')), parts along dimension 0
- core_tensor: float32 [128, 64, 32], P('groups'), parts along dimension 0
There are 2 independent parts, one for each index of `groups`. A program takes and returns all parts, laid end to end along the dimension named above; each array names one. Nothing has to cross between parts.
All inputs are finite; a program needn't handle non-finite values.
Results may differ from a plain program's by a relative error of at most 0.0001.
Values sent between devices are 32-bit elements; how exact they have to be, the bound alone decides.
No kernel may reach another device: no remote copies, remote signals or barrier semaphores. Data moves between devices by JAX's collectives and lax.ppermute only.
A program may use at most 64 MiB of HBM per device.

v0:
```python
import functools
import math

import jax
import jax.numpy as jnp
from jax import lax
from jax.sharding import PartitionSpec as P

NEWTON = 3


exact_mode = lax.Precision.HIGHEST


def cut_along(shard, dim, peers):
    dims = shard.shape
    pieces = shard.reshape(*dims[:dim], peers, dims[dim] // peers, *dims[dim + 1 :])
    return jnp.moveaxis(pieces, dim, 0)


def sum_at_owner(shard, axis, dim):
    peers = lax.axis_size(axis)
    pieces = lax.all_to_all(cut_along(shard, dim, peers), axis, 0, 0, tiled=True)
    return jnp.sum(pieces, axis=0)


def sent_to_all(shard, axis):
    peers = lax.axis_size(axis)
    return lax.all_to_all(
        jnp.broadcast_to(shard[None], (peers, *shard.shape)), axis, 0, 0, tiled=True
    )


def of_everyone(shard, axis):
    return sent_to_all(shard, axis).sum(axis=0)


def padded_to(lines, peers):
    spare = -lines.shape[0] % peers
    if not spare:
        return lines
    return jnp.concatenate([lines, jnp.zeros((spare, *lines.shape[1:]), lines.dtype)])


def nested_sum(shard, near, far):
    lines = shard.reshape(-1, *shard.shape[1:][-1:])
    padded = padded_to(lines, lax.axis_size(near))
    own = lax.psum_scatter(padded, near, scatter_dimension=0, tiled=True)
    own = lax.psum(own, far)
    whole = lax.all_gather(own, near, axis=0, tiled=True)
    return whole[: len(lines)].reshape(shard.shape)


def by_axis(shard, axes):
    return functools.reduce(lax.psum, axes, shard)


def newton_steps(matrix, reduce_gram):
    gram_matrix = reduce_gram(jnp.dot(matrix.T, matrix, precision=exact_mode))
    total = jnp.trace(gram_matrix) + 1e-06
    current = matrix / jnp.sqrt(total)
    gram_matrix = gram_matrix / total
    identity = jnp.eye(matrix.shape[1], dtype=jnp.float32)
    for newton_index in range(NEWTON):
        if newton_index > 0:
            gram_matrix = reduce_gram(jnp.dot(current.T, current, precision=exact_mode))
        current = jnp.dot(current, 1.5 * identity - 0.5 * gram_matrix, precision=exact_mode)
    return current


def body(tensor, start_one, start_two, start_three):
    first, second, third = (start_one, start_two, start_three)
    block_one, block_two, block_three = tensor.shape
    rank_one = first.shape[1]
    rank_two = second.shape[1]
    rank_three = third.shape[1]
    core_flat = None
    sectioned = jnp.einsum("ijk,jb->bik", tensor, second, precision=exact_mode)
    unfolded = jnp.einsum("bik,kc->ibc", sectioned, third, precision=exact_mode).reshape(
        block_one, rank_two * rank_three
    )
    share = sum_at_owner(unfolded, ("cols", "depth"), 1)
    piece = of_everyone(jnp.dot(first.T, share, precision=exact_mode), "rows")
    z_part = jnp.dot(share, piece.T, precision=exact_mode)
    z_rows = of_everyone(z_part, ("cols", "depth"))
    first = newton_steps(z_rows, lambda matrix: of_everyone(matrix, "rows"))
    sectioned = jnp.einsum("ijk,ia->ajk", tensor, first, precision=exact_mode)
    unfolded = jnp.einsum("ajk,kc->jac", sectioned, third, precision=exact_mode).reshape(
        block_two, rank_one * rank_three
    )
    share = sum_at_owner(unfolded, ("rows", "depth"), 1)
    piece = of_everyone(jnp.dot(second.T, share, precision=exact_mode), "cols")
    z_part = jnp.dot(share, piece.T, precision=exact_mode)
    z_rows = of_everyone(z_part, ("rows", "depth"))
    second = newton_steps(z_rows, lambda matrix: of_everyone(matrix, "cols"))
    unfolded = jnp.einsum("ajk,jb->kab", sectioned, second, precision=exact_mode).reshape(
        block_three, rank_one * rank_two
    )
    core_flat = nested_sum(
        jnp.dot(third.T, unfolded, precision=exact_mode), "depth", ("rows", "cols")
    )
    z_rows = by_axis(jnp.dot(unfolded, core_flat.T, precision=exact_mode), ("rows", "cols"))
    third = newton_steps(z_rows, lambda matrix: of_everyone(matrix, "depth"))
    core_tensor = core_flat.reshape(rank_three, rank_one, rank_two).transpose(1, 2, 0)
    length_one = block_one * lax.axis_size("rows")
    length_two = block_two * lax.axis_size("cols")
    length_three = block_three * lax.axis_size("depth")
    return (
        first * math.sqrt(length_one),
        second * math.sqrt(length_two),
        third * math.sqrt(length_three),
        core_tensor,
    )


def solution(mesh):
    in_specs = (
        P(("groups", "rows"), "cols", "depth"),
        P(("groups", "rows"), None),
        P(("groups", "cols"), None),
        P(("groups", "depth"), None),
    )
    out_specs = (
        P(("groups", "rows"), None),
        P(("groups", "cols"), None),
        P(("groups", "depth"), None),
        P("groups", None, None),
    )
    return jax.shard_map(body, mesh=mesh, in_specs=in_specs, out_specs=out_specs, check_vma=False)
```

profile of v0, /device:TPU:65, one launch (start us, length us, event | category | flops | bytes accessed | tf_op | source)
XLA Modules:
  0.0 697.6 jit_solution(12979752503922956730)
XLA Ops:
  7.3 0.8 copy-done
  8.1 1.3 fusion.51
  9.4 1.5 convolution_bitcast_fusion.2
  11.3 53.1 %all_to_all.75 = f32[16,16,128]{2,1,0:T(8,128)S(1)} all-to-all(f32[16,16,128]{2,1,0:T(8,128)S(1)} %copy.34), channel_id=1, replica_groups=mesh['groups'=2,'rows'=16,'cols'=8,'depth'=2] {'cols','depth'}, dimensions={0} | all-to-all | bytes 262144 | tf_op jit(solution)/shard_map/all_to_all | solution.py:23
  64.5 0.2 convolution_bitcast_fusion.4
  64.8 31.9 %all_to_all.76 = f32[16,64,128]{2,1,0:T(8,128)S(1)} all-to-all(f32[16,64,128]{2,1,0:T(8,128)S(1)} %broadcast_in_dim.34), channel_id=1, replica_groups=mesh['groups'=2,'rows'=16,'cols'=8,'depth'=2] {'rows'}, dimensions={0} | all-to-all | bytes 1048576 | tf_op jit(solution)/shard_map/all_to_all | solution.py:29
  97.0 15.4 %all_to_all.77 = f32[16,1,1024]{2,1,0:T(1,128)S(1)} all-to-all(f32[16,1,1024]{2,1,0:T(1,128)S(1)} %reshape.33), channel_id=1, replica_groups=mesh['groups'=2,'rows'=16,'cols'=8,'depth'=2] {'cols','depth'}, dimensions={0} | all-to-all | bytes 131072 | tf_op jit(solution)/shard_map/all_to_all | solution.py:29
  112.4 0.5 broadcast.111
  112.9 0.8 reduce
  113.8 0.2 fusion.96
  114.1 0.3 reshape.35
  114.4 20.3 %all_to_all.78 = f32[16,1,4096]{2,1,0:T(1,128)S(1)} all-to-all(f32[16,1,4096]{2,1,0:T(1,128)S(1)} %reshape.35), channel_id=1, replica_groups=mesh['groups'=2,'rows'=16,'cols'=8,'depth'=2] {'rows'}, dimensions={0} | all-to-all | bytes 524288 | tf_op jit(solution)/shard_map/all_to_all | solution.py:29
  134.8 1.3 reduce.1
  136.0 0.2 reshape.36
  136.3 0.6 select_reduce_fusion.1
  137.8 0.2 fusion.97
  138.1 0.3 reshape.37
  138.4 23.7 %all_to_all.79 = f32[16,1,4096]{2,1,0:T(1,128)S(1)} all-to-all(f32[16,1,4096]{2,1,0:T(1,128)S(1)} %reshape.37), channel_id=1, replica_groups=mesh['groups'=2,'rows'=16,'cols'=8,'depth'=2] {'rows'}, dimensions={0} | all-to-all | bytes 524288 | tf_op jit(solution)/shard_map/all_to_all | solution.py:29
  162.1 1.3 reduce.2
  163.4 0.2 reshape.38
  163.8 0.2 fusion.98
  164.1 0.3 reshape.39
  164.5 23.9 %all_to_all.80 = f32[16,1,4096]{2,1,0:T(1,128)S(1)} all-to-all(f32[16,1,4096]{2,1,0:T(1,128)S(1)} %reshape.39), channel_id=1, replica_groups=mesh['groups'=2,'rows'=16,'cols'=8,'depth'=2] {'rows'}, dimensions={0} | all-to-all | bytes 524288 | tf_op jit(solution)/shard_map/all_to_all | solution.py:29
  188.4 1.3 reduce.3
  189.9 0.8 broadcast_multiply_fusion.1
  190.7 0.6 fusion.4
  191.3 0.8 convolution_bitcast_fusion.1
  192.8 27.0 %all_to_all.81 = f32[32,1,1024]{2,1,0:T(1,128)S(1)} all-to-all(f32[32,1,1024]{2,1,0:T(1,128)S(1)} %reshape.41), channel_id=1, replica_groups=mesh['groups'=2,'rows'=16,'cols'=8,'depth'=2] {'rows','depth'}, dimensions={0} | all-to-all | bytes 262144 | tf_op jit(solution)/shard_map/all_to_all | solution.py:23
  219.8 1.0 reduce.4
  220.9 0.2 convolution_bitcast_fusion.3
  221.4 10.4 %all_to_all.82 = f32[8,1,4096]{2,1,0:T(1,128)S(1)} all-to-all(f32[8,1,4096]{2,1,0:T(1,128)S(1)} %reshape.43), channel_id=1, replica_groups=mesh['groups'=2,'rows'=16,'cols'=8,'depth'=2] {'cols'}, dimensions={0} | all-to-all | bytes 262144 | tf_op jit(solution)/shard_map/all_to_all | solution.py:29
  231.8 1.0 reduce.5
  233.3 21.6 %all_to_all.83 = f32[32,1,1024]{2,1,0:T(1,128)S(1)} all-to-all(f32[32,1,1024]{2,1,0:T(1,128)S(1)} %reshape.45), channel_id=1, replica_groups=mesh['groups'=2,'rows'=16,'cols'=8,'depth'=2] {'rows','depth'}, dimensions={0} | all-to-all | bytes 262144 | tf_op jit(solution)/shard_map/all_to_all | solution.py:29
  254.8 1.0 reduce.6
  255.9 0.2 fusion.100
  256.4 10.4 %all_to_all.84 = f32[8,1,4096]{2,1,0:T(1,128)S(1)} all-to-all(f32[8,1,4096]{2,1,0:T(1,128)S(1)} %reshape.47), channel_id=1, replica_groups=mesh['groups'=2,'rows'=16,'cols'=8,'depth'=2] {'cols'}, dimensions={0} | all-to-all | bytes 262144 | tf_op jit(solution)/shard_map/all_to_all | solution.py:29
  266.8 1.0 reduce.7
  267.9 0.6 select_reduce_fusion
  269.3 0.2 fusion.101
  269.8 10.4 %all_to_all.85 = f32[8,1,4096]{2,1,0:T(1,128)S(1)} all-to-all(f32[8,1,4096]{2,1,0:T(1,128)S(1)} %reshape.49), channel_id=1, replica_groups=mesh['groups'=2,'rows'=16,'cols'=8,'depth'=2] {'cols'}, dimensions={0} | all-to-all | bytes 262144 | tf_op jit(solution)/shard_map/all_to_all | solution.py:29
  280.2 1.0 reduce.8
  281.4 0.2 fusion.102
  281.9 10.4 %all_to_all.86 = f32[8,1,4096]{2,1,0:T(1,128)S(1)} all-to-all(f32[8,1,4096]{2,1,0:T(1,128)S(1)} %reshape.51), channel_id=1, replica_groups=mesh['groups'=2,'rows'=16,'cols'=8,'depth'=2] {'cols'}, dimensions={0} | all-to-all | bytes 262144 | tf_op jit(solution)/shard_map/all_to_all | solution.py:29
  292.2 1.0 reduce.9
  293.3 0.8 broadcast_multiply_fusion
  294.1 1.9 fusion.1
  296.0 3.0 convolution_bitcast_fusion
  299.1 14.5 %reduce-scatter.2.cloned.1.call-done = f32[16,4096]{1,0:T(8,128)} async-done(((f32[32,4096]{1,0:T(8,128)}), f32[16,4096]{1,0:T(8,128)}) %reduce-scatter.2.cloned.1.call-update) | async-done | bytes 262160 | tf_op jit(solution)/shard_map/reduce_scatter | solution.py:48
  313.6 260.9 %all-reduce.2.cloned.1.call-done = f32[16,4096]{1,0:T(8,128)} async-done(((f32[16,4096]{1,0:T(8,128)}), f32[16,4096]{1,0:T(8,128)}) %all-reduce.2.cloned.1.call-update) | async-done | bytes 262160 | tf_op jit(solution)/shard_map/psum | solution.py:49
  574.6 13.2 %all_gather.3 = f32[32,4096]{1,0:T(8,128)S(1)} all-gather(f32[16,4096]{1,0:T(8,128)} %all-reduce.2.cloned.1.call-done), channel_id=1, replica_groups=mesh['groups'=2,'rows'=16,'cols'=8,'depth'=2] {'depth'}, dimensions={0}, use_global_device_ids=true | all-gather | bytes 786432 | tf_op jit(solution)/shard_map/all_gather | solution.py:50
  587.8 1.3 fusion.103
  589.1 0.4 reshape.28
  589.5 39.6 %psum.22 = f32[128,32]{0,1:T(8,128)S(1)} all-reduce(f32[128,32]{0,1:T(8,128)S(1)} %fusion.103), channel_id=1, replica_groups=mesh['groups'=2,'rows'=16,'cols'=8,'depth'=2] {'rows'}, use_global_device_ids=true, to_apply=%region_16.17 | all-reduce | flops 4096 | bytes 32768 | tf_op jit(solution)/shard_map/psum | solution.py:55
  629.2 22.4 %psum.23 = f32[128,32]{0,1:T(8,128)S(1)} all-reduce(f32[128,32]{0,1:T(8,128)S(1)} %psum.22), channel_id=1, replica_groups=mesh['groups'=2,'rows'=16,'cols'=8,'depth'=2] {'cols'}, use_global_device_ids=true, to_apply=%region_17.18 | all-reduce | flops 4096 | bytes 32768 | tf_op jit(solution)/shard_map/psum | solution.py:55
  651.8 24.5 %all_to_all.87 = f32[2,1,1024]{2,1,0:T(1,128)S(1)} all-to-all(f32[2,1,1024]{2,1,0:T(1,128)S(1)} %reshape.53), channel_id=1, replica_groups=mesh['groups'=2,'rows'=16,'cols'=8,'depth'=2] {'depth'}, dimensions={0} | all-to-all | bytes 16384 | tf_op jit(solution)/shard_map/all_to_all | solution.py:29
  676.3 0.7 reduce.10
  677.1 0.6 select_reduce_fusion.2
  678.4 0.2 fusion.20
  678.9 3.7 all_to_all.88
  682.6 0.7 reduce.11
  683.8 3.7 all_to_all.89
  687.6 0.7 reduce.12
  688.3 0.8 convolution_multiply_fusion
  689.2 1.6 copy.51
  (77 shorter events, 6.1 us)
Async XLA Ops:
  7.2 0.9 copy-start
  7.2 57.3 %copy-start.3 = (f32[16,64]{1,0:T(8,128)S(1)}, f32[16,64]{1,0:T(8,128)}, u32[]{:S(2)}) copy-start(f32[16,64]{1,0:T(8,128)} %param.5) | copy-start | bytes 12292
  7.2 306.4 %reduce-scatter.2.cloned.1.call-start = ((), (), s32[]{:S(2)}) async-start(), calls=%async_computation.16 | async-start | bytes 786432 | tf_op jit(solution)/shard_map/reduce_scatter | solution.py:48
  164.1 27.2 %copy-start.1 = (f32[128,32]{0,1:T(8,128)S(1)}, f32[128,32]{0,1:T(8,128)}, u32[]{:S(2)}) copy-start(f32[128,32]{0,1:T(8,128)} %param.7) | copy-start | bytes 49156
  192.1 28.8 %copy-start.2 = (f32[16,64]{1,0:T(8,128)S(1)}, f32[16,64]{1,0:T(8,128)}, u32[]{:S(2)}) copy-start(f32[16,64]{1,0:T(8,128)} %param.6) | copy-start | bytes 12292
  299.0 275.6 %all-reduce.2.cloned.1.call-start = ((), (), s32[]{:S(2)}) async-start(), calls=%async_computation.17 | async-start | bytes 524288 | tf_op jit(solution)/shard_map/psum | solution.py:49
Sparse Core Ops, SparseCore 0:
  299.1 14.4 reduce-scatter.1
  317.1 257.4 all-reduce.1
where the time goes:
time: 699 us; the launch traced here: 698 us
  blocking collectives  366 us (52%)
  waiting for transfers between devices  276 us (39%)
  between operations  16.8 us (2%)
  matrix products  16.4 us (2%)
  other arithmetic  14.6 us (2%)
  local copies, waits for them, and re-layouts  8.63 us (1%)
    psum x1, waiting for transfers between devices, nested_sum(): own = lax.psum(own, far)  261 us
    all_to_all x13, blocking collectives, sent_to_all(): lax.all_to_all(jnp.broadcast_to(shard[None], (peers, *shard.shape)), axis...  210 us
    all_to_all x2, blocking collectives, sum_at_owner(): lax.all_to_all(cut_along(shard, dim, peers), axis, 0, 0, tiled=True)  80.1 us
    psum x2, blocking collectives, by_axis(): return functools.reduce(lax.psum, axes, shard)  62 us
    reduce_scatter x1, waiting for transfers between devices, nested_sum(): own = lax.psum_scatter(padded, near, scatter_dimension=0, tiled=True)  14.5 us
  transfers between devices with their start and end apart: 2, of which 2 were waited for; matrix products, arithmetic and copies ran while one was open for 0% of the time, Pallas kernels for 0%

commit v1 on v0

v1 whole, which is shorter than its diff:
```python
import math

import jax
import jax.numpy as jnp
from jax import lax
from jax.sharding import PartitionSpec as P

NEWTON = 3
LANES = 128
exact_mode = lax.Precision.HIGHEST


def mul(left, right):
    return jnp.dot(left, right, precision=exact_mode)


def from_everyone(shard, axis):
    peers = lax.axis_size(axis)
    return lax.all_to_all(
        jnp.broadcast_to(shard[None], (peers, *shard.shape)), axis, 0, 0, tiled=True
    )


def orth_factor(gram):
    total = jnp.trace(gram) + 1e-06
    gram = gram / total
    identity = jnp.eye(gram.shape[0], dtype=jnp.float32)
    factor = None
    for step in range(NEWTON):
        move = 1.5 * identity - 0.5 * gram
        factor = move if factor is None else mul(factor, move)
        if step + 1 < NEWTON:
            gram = mul(mul(move, gram), move)
    return factor / jnp.sqrt(total)


def halves_side_by_side(block):
    half = block.shape[0] // 2
    return jnp.concatenate([block[:half], block[half:]], axis=1)


def halves_stacked(blocks):
    count, half, width = blocks.shape
    width //= 2
    pairs = jnp.stack([blocks[:, :, :width], blocks[:, :, width:]], axis=1)
    return pairs.reshape(count * 2 * half, width)


def body(tensor, start_one, start_two, start_three):
    size_one, size_two, size_three = tensor.shape
    rank_one = start_one.shape[1]
    rank_two = start_two.shape[1]
    rank_three = start_three.shape[1]
    rows, cols, depth = (lax.axis_size(name) for name in ("rows", "cols", "depth"))
    row, col, level = (lax.axis_index(name) for name in ("rows", "cols", "depth"))
    length_one, length_two, length_three = size_one * rows, size_two * cols, size_three * depth
    owners = cols * depth
    slices = rank_three // owners
    flat = tensor.reshape(size_one * size_two, size_three)

    thinned = lax.dot_general(
        start_three, flat, (((0,), (1,)), ((), ())), precision=exact_mode
    ).reshape(owners, -1, LANES)
    two_packed = halves_side_by_side(start_two)
    part = two_packed.shape[0] // depth
    two_part = lax.dynamic_slice_in_dim(two_packed, level * part, part, 0)
    lines = thinned.shape[1]
    message = jnp.concatenate(
        [thinned, jnp.broadcast_to(two_part[None], (owners, *two_part.shape))], axis=1
    )
    got = lax.all_to_all(message, ("cols", "depth"), 0, 0, tiled=True)
    got = got.reshape(cols, depth, *got.shape[1:])
    own = got[:, :, :lines].sum(axis=1).reshape(cols, slices * size_one, size_two)
    own = own.transpose(1, 0, 2).reshape(slices * size_one, length_two)
    two_old = halves_stacked(got[:, :, lines:].reshape(cols, depth * part, 2 * rank_two))

    message = jnp.concatenate([own, halves_side_by_side(start_one)], axis=0)
    got = from_everyone(message, "rows")
    whole = [
        got[:, c * size_one : (c + 1) * size_one].reshape(length_one, length_two)
        for c in range(slices)
    ]
    one_old = halves_stacked(got[:, slices * size_one :])

    unfolded = jnp.concatenate([mul(matrix, two_old) for matrix in whole], axis=1)
    core = mul(one_old.T, unfolded)
    z_part = mul(core, unfolded.T)
    z_part = lax.all_gather(z_part, "depth").sum(axis=0)
    z_one = from_everyone(z_part, "cols").sum(axis=0)
    one = mul(orth_factor(mul(z_one, z_one.T)), z_one)

    projected = jnp.concatenate([mul(one, matrix) for matrix in whole], axis=0)
    projected = from_everyone(projected, "cols").reshape(-1, length_two)
    core = mul(projected, two_old)
    z_part = mul(core.T, projected)
    z_two = lax.all_gather(z_part, "depth").sum(axis=0)
    two = mul(orth_factor(mul(z_two, z_two.T)), z_two)

    one_own = lax.dynamic_slice_in_dim(one, row * size_one, size_one, 1)
    two_own = lax.dynamic_slice_in_dim(two, col * size_two, size_two, 1)
    core = mul(two, projected.T)
    grid = projected.reshape(-1, rank_one, length_two)
    spread = jnp.einsum("ai,caj->cij", one_own, grid, precision=exact_mode)
    spread = mul(spread.reshape(-1, length_two), mul(two.T, two_own))
    spread = spread.reshape(-1, size_one * size_two)
    core = lax.all_gather(core, "depth")
    spread = lax.all_gather(spread, "depth")
    spread = spread.reshape(depth, cols, slices, -1).transpose(1, 0, 2, 3).reshape(rank_three, -1)
    z_part = mul(spread, flat)
    z_part = from_everyone(z_part, "cols").sum(axis=0)
    z_three = from_everyone(z_part, "rows").sum(axis=0)
    gram = lax.all_gather(mul(z_three, z_three.T), "depth").sum(axis=0)
    three = mul(orth_factor(gram), z_three)

    core = core.reshape(depth, rank_two, cols, slices, rank_one)
    core = core.transpose(4, 1, 2, 0, 3).reshape(rank_one, rank_two, rank_three)
    return (
        one_own.T * math.sqrt(length_one),
        two_own.T * math.sqrt(length_two),
        three.T * math.sqrt(length_three),
        core,
    )


def solution(mesh):
    in_specs = (
        P(("groups", "rows"), "cols", "depth"),
        P(("groups", "rows"), None),
        P(("groups", "cols"), None),
        P(("groups", "depth"), None),
    )
    out_specs = (
        P(("groups", "rows"), None),
        P(("groups", "cols"), None),
        P(("groups", "depth"), None),
        P("groups", None, None),
    )
    return jax.shard_map(body, mesh=mesh, in_specs=in_specs, out_specs=out_specs, check_vma=False)
```

time: 699 us -> 186 us (0.27)
  blocking collectives: 366 us -> 56.7 us
  waiting for transfers between devices: 276 us -> 43.3 us
  starting transfers between devices: 0.13 us -> 61.6 us
  between operations: 16.8 us -> 3.14 us
  other arithmetic: 14.6 us -> 1.73 us
    psum x1 -> x0, waiting for transfers between devices: 261 us -> none  [nested_sum(): own = lax.psum(own, far)]
    all_to_all x15 -> x2, blocking collectives: 290 us -> 31.2 us  [from_everyone(): lax.all_to_all(jnp.broadcast_to(shard[None], (peers, *shard.shape)), axis...]
    psum x2 -> x0, blocking collectives: 62 us -> none  [by_axis(): return functools.reduce(lax.psum, axes, shard)]
    all_to_all x0 -> x4, starting transfers between devices: none -> 61.6 us  [the longest x1 44.9 us: body(): got = lax.all_to_all(message, ('cols', 'depth'), 0, 0, tiled=True)]
    all_to_all x0 -> x4, waiting for transfers between devices: none -> 43.3 us  [the longest x3 35.4 us: from_everyone(): lax.all_to_all(jnp.broadcast_to(shard[None], (peers, *shard.shape)), axis...]
    reduce_scatter x1 -> x0, waiting for transfers between devices: 14.5 us -> none  [nested_sum(): own = lax.psum_scatter(padded, near, scatter_dimension=0, tiled=True)]
    all_to_all x13 -> x0, other arithmetic: 12.3 us -> none  [the longest x12 11.4 us: sent_to_all(): lax.all_to_all(jnp.broadcast_to(shard[None], (peers, *shard.shape)), axis...]
    all_gather x1 -> x5, blocking collectives: 13.2 us -> 25.5 us  [the longest x1 8.43 us: body(): gram = lax.all_gather(mul(z_three, z_three.T), 'depth').sum(axis=0)]
  transfers between devices with their start and end apart: 2 -> 4, of which waited for: 2 -> 4; matrix products, arithmetic and copies ran while one was open for 0% -> 3% of each run, Pallas kernels for 0% -> 0%
where the time goes in v1:
time: 186 us; the launch traced here: 185 us
  starting transfers between devices  61.6 us (33%)
  blocking collectives  56.7 us (30%)
  waiting for transfers between devices  43.3 us (23%)
  matrix products  10.5 us (6%)
  local copies, waits for them, and re-layouts  8.09 us (4%)
  between operations  3.14 us (2%)
    all_to_all x1, starting transfers between devices, body(): got = lax.all_to_all(message, ('cols', 'depth'), 0, 0, tiled=True)  44.9 us
    all_to_all x3, waiting for transfers between devices, from_everyone(): lax.all_to_all(jnp.broadcast_to(shard[None], (peers, *shard.shape)), axis...  35.4 us
    all_to_all x2, blocking collectives, from_everyone(): lax.all_to_all(jnp.broadcast_to(shard[None], (peers, *shard.shape)), axis...  31.2 us
    all_to_all x3, starting transfers between devices, from_everyone(): lax.all_to_all(jnp.broadcast_to(shard[None], (peers, *shard.shape)), axis...  16.8 us
    dot_general x36, matrix products, mul(): return jnp.dot(left, right, precision=exact_mode)  9.84 us
    all_gather x1, blocking collectives, body(): gram = lax.all_gather(mul(z_three, z_three.T), 'depth').sum(axis=0)  8.43 us
    all_gather x1, blocking collectives, body(): z_part = lax.all_gather(z_part, 'depth').sum(axis=0)  8.08 us
    all_to_all x1, waiting for transfers between devices, body(): got = lax.all_to_all(message, ('cols', 'depth'), 0, 0, tiled=True)  7.9 us
  transfers between devices with their start and end apart: 4, of which 4 were waited for; matrix products, arithmetic and copies ran while one was open for 3% of the time, Pallas kernels for 0%

profile of v1, /device:TPU:65, one launch (start us, length us, event | category | flops | bytes accessed | tf_op | source)
XLA Modules:
  0.0 185.2 jit_solution(7530526589334010216)
XLA Ops:
  0.7 0.7 copy-done.2
  1.4 0.2 copy-done
  1.6 0.2 fusion.120
  1.9 0.6 pad_maximum_fusion.4
  2.6 44.9 %all-to-all-start = ((f32[16,8,128]{2,1,0:T(8,128)}), f32[16,8,128]{2,1,0:T(8,128)S(1)}, u32[]{:S(2)}, u32[]{:S(2)}) async-start(f32[16,8,128]{2,1,0:T(8,128)} %pad_maximum_fusion.4), calls=%async_computation | async-start | bytes 131072 | tf_op jit(solution)/shard_map/all_to_all | solution.py:71
  47.5 7.9 %all-to-all-done = f32[16,8,128]{2,1,0:T(8,128)S(1)} async-done(((f32[16,8,128]{2,1,0:T(8,128)}), f32[16,8,128]{2,1,0:T(8,128)S(1)}, u32[]{:S(2)}, u32[]{:S(2)}) %all-to-all-start) | async-done | bytes 65568 | tf_op jit(solution)/shard_map/all_to_all | solution.py:71
  55.7 0.8 broadcast_in_dim.17
  56.5 7.3 %all-to-all-start.1 = ((f32[16,40,128]{2,1,0:T(8,128)}), f32[16,40,128]{2,1,0:T(8,128)S(1)}, u32[]{:S(2)}, u32[]{:S(2)}) async-start(f32[16,40,128]{2,1,0:T(8,128)} %broadcast_in_dim.17), calls=%async_computation.1 | async-start | bytes 655360 | tf_op jit(solution)/shard_map/all_to_all | solution.py:19
  63.9 15.3 %all-to-all-done.1 = f32[16,40,128]{2,1,0:T(8,128)S(1)} async-done(((f32[16,40,128]{2,1,0:T(8,128)}), f32[16,40,128]{2,1,0:T(8,128)S(1)}, u32[]{:S(2)}, u32[]{:S(2)}) %all-to-all-start.1) | async-done | bytes 327712 | tf_op jit(solution)/shard_map/all_to_all | solution.py:19
  79.2 0.3 fusion.122
  79.5 0.3 fusion.121
  79.9 0.4 fusion.4
  80.2 0.2 fusion.3
  80.4 8.1 %all-gather = f32[128,256]{1,0:T(8,128)S(1)} all-gather(f32[64,256]{1,0:T(8,128)S(1)} %fusion.3), channel_id=2, replica_groups=mesh['groups'=2,'rows'=16,'cols'=8,'depth'=2] {'depth'}, dimensions={0}, use_global_device_ids=true | all-gather | bytes 196608 | tf_op jit(solution)/shard_map/all_gather | solution.py:88
  88.6 20.4 %all_to_all.30 = f32[8,64,256]{2,1,0:T(8,128)S(1)} all-to-all(f32[8,64,256]{2,1,0:T(8,128)S(1)} %broadcast_in_dim.18), channel_id=1, replica_groups=mesh['groups'=2,'rows'=16,'cols'=8,'depth'=2] {'cols'}, dimensions={0} | all-to-all | bytes 1048576 | tf_op jit(solution)/shard_map/all_to_all | solution.py:19
  109.0 0.8 select_reduce_fusion.1
  110.5 0.2 fusion.14
  110.7 0.2 fusion.13
  110.9 0.2 fusion.12
  111.1 0.2 fusion.11
  111.2 0.2 fusion.1
  111.4 0.2 convolution_divide_fusion.1
  111.6 0.2 fusion.123
  111.8 0.2 fusion.125
  112.0 0.2 fusion.124
  112.2 0.8 broadcast_in_dim.19
  113.1 3.7 %all-to-all-start.3 = ((f32[8,128,128]{2,1,0:T(8,128)}), f32[8,128,128]{2,1,0:T(8,128)S(1)}, u32[]{:S(2)}, u32[]{:S(2)}) async-start(f32[8,128,128]{2,1,0:T(8,128)} %broadcast_in_dim.19), calls=%async_computation.3 | async-start | bytes 1048576 | tf_op jit(solution)/shard_map/all_to_all | solution.py:19
  116.8 16.4 %all-to-all-done.3 = f32[8,128,128]{2,1,0:T(8,128)S(1)} async-done(((f32[8,128,128]{2,1,0:T(8,128)}), f32[8,128,128]{2,1,0:T(8,128)S(1)}, u32[]{:S(2)}, u32[]{:S(2)}) %all-to-all-start.3) | async-done | bytes 524320 | tf_op jit(solution)/shard_map/all_to_all | solution.py:19
  133.2 0.7 fusion.126
  133.9 0.4 fusion.127
  134.4 3.3 %all-gather.1 = f32[128,128]{1,0:T(8,128)S(1)} all-gather(f32[64,128]{1,0:T(8,128)S(1)} %fusion.127), channel_id=3, replica_groups=mesh['groups'=2,'rows'=16,'cols'=8,'depth'=2] {'depth'}, dimensions={0}, use_global_device_ids=true | all-gather | bytes 98304 | tf_op jit(solution)/shard_map/all_gather | solution.py:96
  137.7 0.8 select_reduce_fusion
  139.2 0.2 fusion.10
  139.3 0.2 fusion.9
  139.5 0.2 fusion.8
  139.7 0.2 fusion.7
  139.9 0.2 fusion
  140.0 0.2 convolution_divide_fusion
  140.2 0.2 fusion.128
  140.4 0.5 fusion.5
  140.8 0.3 fusion.15
  141.1 0.3 fusion.129
  141.5 1.9 %all_gather.31 = f32[2,16,256]{2,1,0:T(8,128)S(1)} all-gather(f32[1,16,256]{2,1,0:T(8,128)S(1)} %all_gather_reshape.3), channel_id=1, replica_groups=mesh['groups'=2,'rows'=16,'cols'=8,'depth'=2] {'depth'}, dimensions={0}, use_global_device_ids=true | all-gather | bytes 49152 | tf_op jit(solution)/shard_map/all_gather | solution.py:107
  143.5 0.2 fusion.130
  143.7 10.8 %all_to_all.31 = f32[8,32,128]{2,1,0:T(8,128)S(1)} all-to-all(f32[8,32,128]{2,1,0:T(8,128)S(1)} %broadcast_in_dim.20), channel_id=1, replica_groups=mesh['groups'=2,'rows'=16,'cols'=8,'depth'=2] {'cols'}, dimensions={0} | all-to-all | bytes 262144 | tf_op jit(solution)/shard_map/all_to_all | solution.py:19
  154.5 0.7 broadcast_in_dim.21
  155.3 5.8 %all-to-all-start.5 = ((f32[16,32,128]{2,1,0:T(8,128)}), f32[16,32,128]{2,1,0:T(8,128)S(1)}, u32[]{:S(2)}, u32[]{:S(2)}) async-start(f32[16,32,128]{2,1,0:T(8,128)} %broadcast_in_dim.21), calls=%async_computation.5 | async-start | bytes 524288 | tf_op jit(solution)/shard_map/all_to_all | solution.py:19
  161.1 0.7 copy.42
  161.9 0.7 copy.43
  162.6 0.7 fusion.132
  163.2 3.8 %all-gather.3 = f32[128,1024]{1,0:T(8,128)S(1)} all-gather(f32[64,1024]{1,0:T(8,128)S(1)} %fusion.132), channel_id=5, replica_groups=mesh['groups'=2,'rows'=16,'cols'=8,'depth'=2] {'depth'}, dimensions={0}, use_global_device_ids=true | all-gather | bytes 786432 | tf_op jit(solution)/shard_map/all_gather | solution.py:106
  167.0 0.8 reshape.76
  167.7 2.1 %copy.41 = f32[64,64,8,2,2]{1,4,3,2,0:T(2,128)} copy(f32[64,64,8,2,2]{0,4,2,1,3:T(2,128)S(1)} %bitcast.98) | data formatting | bytes 1048576 | tf_op jit(solution)/shard_map/transpose | solution.py:116
  169.9 3.7 %all-to-all-done.5 = f32[16,32,128]{2,1,0:T(8,128)S(1)} async-done(((f32[16,32,128]{2,1,0:T(8,128)}), f32[16,32,128]{2,1,0:T(8,128)S(1)}, u32[]{:S(2)}, u32[]{:S(2)}) %all-to-all-start.5) | async-done | bytes 262176 | tf_op jit(solution)/shard_map/all_to_all | solution.py:19
  173.6 0.1 fusion.131
  173.7 8.4 %all-gather.2 = f32[64,32]{1,0:T(8,128)S(1)} all-gather(f32[32,32]{1,0:T(8,128)S(1)} %fusion.131), channel_id=4, replica_groups=mesh['groups'=2,'rows'=16,'cols'=8,'depth'=2] {'depth'}, dimensions={0}, use_global_device_ids=true | all-gather | bytes 12288 | tf_op jit(solution)/shard_map/all_gather | solution.py:112
  182.2 0.6 select_reduce_fusion.2
  183.5 0.1 fusion.21
  183.6 0.2 fusion.20
  183.8 0.1 fusion.19
  183.9 0.1 fusion.18
  184.1 0.2 fusion.2
  184.3 0.1 convolution_divide_fusion.2
  184.4 0.8 convolution_multiply_fusion.2
  (37 shorter events, 1.2 us)
Async XLA Ops:
  0.6 0.9 copy-start
  0.6 0.7 copy-start.2
  0.7 0.9 copy-start.1
  2.6 44.9 %copy-start.3 = (f32[16,64]{1,0:T(8,128)S(1)}, f32[16,64]{1,0:T(8,128)}, u32[]{:S(2)}) copy-start(f32[16,64]{1,0:T(8,128)} %param.5) | copy-start | bytes 12292
  2.6 52.8 %all-to-all-start = ((f32[16,8,128]{2,1,0:T(8,128)}), f32[16,8,128]{2,1,0:T(8,128)S(1)}, u32[]{:S(2)}, u32[]{:S(2)}) async-start(f32[16,8,128]{2,1,0:T(8,128)} %pad_maximum_fusion.4), calls=%async_computation | async-start | bytes 131072 | tf_op jit(solution)/shard_map/all_to_all | solution.py:71
  56.5 22.7 %all-to-all-start.1 = ((f32[16,40,128]{2,1,0:T(8,128)}), f32[16,40,128]{2,1,0:T(8,128)S(1)}, u32[]{:S(2)}, u32[]{:S(2)}) async-start(f32[16,40,128]{2,1,0:T(8,128)} %broadcast_in_dim.17), calls=%async_computation.1 | async-start | bytes 655360 | tf_op jit(solution)/shard_map/all_to_all | solution.py:19
  113.1 20.1 %all-to-all-start.3 = ((f32[8,128,128]{2,1,0:T(8,128)}), f32[8,128,128]{2,1,0:T(8,128)S(1)}, u32[]{:S(2)}, u32[]{:S(2)}) async-start(f32[8,128,128]{2,1,0:T(8,128)} %broadcast_in_dim.19), calls=%async_computation.3 | async-start | bytes 1048576 | tf_op jit(solution)/shard_map/all_to_all | solution.py:19
  155.3 18.3 %all-to-all-start.5 = ((f32[16,32,128]{2,1,0:T(8,128)}), f32[16,32,128]{2,1,0:T(8,128)S(1)}, u32[]{:S(2)}, u32[]{:S(2)}) async-start(f32[16,32,128]{2,1,0:T(8,128)} %broadcast_in_dim.21), calls=%async_computation.5 | async-start | bytes 524288 | tf_op jit(solution)/shard_map/all_to_all | solution.py:19

commit v2 on v1

--- a/solution.py
+++ b/solution.py
@@ -21,10 +21,16 @@
     )
 
 
+def alone(operation, shard, *others):
+    shard, others = lax.optimization_barrier((shard, others))
+    return lax.optimization_barrier((operation(shard), *others))
+
+
 def orth_factor(gram):
-    total = jnp.trace(gram) + 1e-06
+    identity = jnp.eye(gram.shape[0], dtype=jnp.float32)
+    ones = jnp.ones_like(gram)
+    total = mul(ones, mul(gram * identity, ones)) + 1e-06
     gram = gram / total
-    identity = jnp.eye(gram.shape[0], dtype=jnp.float32)
     factor = None
     for step in range(NEWTON):
         move = 1.5 * identity - 0.5 * gram
@@ -52,7 +58,9 @@
     rank_two = start_two.shape[1]
     rank_three = start_three.shape[1]
     rows, cols, depth = (lax.axis_size(name) for name in ("rows", "cols", "depth"))
-    row, col, level = (lax.axis_index(name) for name in ("rows", "cols", "depth"))
+    level = lax.axis_index("depth")
+    row_from = lax.axis_index("rows") * size_one
+    col_from = lax.axis_index("cols") * size_two
     length_one, length_two, length_three = size_one * rows, size_two * cols, size_three * depth
     owners = cols * depth
     slices = rank_three // owners
@@ -68,14 +76,20 @@
     message = jnp.concatenate(
         [thinned, jnp.broadcast_to(two_part[None], (owners, *two_part.shape))], axis=1
     )
-    got = lax.all_to_all(message, ("cols", "depth"), 0, 0, tiled=True)
+    one_packed = halves_side_by_side(start_one)
+    got, one_packed, flat, row_from, col_from = alone(
+        lambda shard: lax.all_to_all(shard, ("cols", "depth"), 0, 0, tiled=True),
+        message, one_packed, flat, row_from, col_from,
+    )
     got = got.reshape(cols, depth, *got.shape[1:])
     own = got[:, :, :lines].sum(axis=1).reshape(cols, slices * size_one, size_two)
     own = own.transpose(1, 0, 2).reshape(slices * size_one, length_two)
     two_old = halves_stacked(got[:, :, lines:].reshape(cols, depth * part, 2 * rank_two))
 
-    message = jnp.concatenate([own, halves_side_by_side(start_one)], axis=0)
-    got = from_everyone(message, "rows")
+    message = jnp.concatenate([own, one_packed], axis=0)
+    got, two_old, flat, row_from, col_from = alone(
+        lambda shard: from_everyone(shard, "rows"), message, two_old, flat, row_from, col_from
+    )
     whole = [
         got[:, c * size_one : (c + 1) * size_one].reshape(length_one, length_two)
         for c in range(slices)
@@ -86,32 +100,42 @@
     core = mul(one_old.T, unfolded)
     z_part = mul(core, unfolded.T)
     z_part = lax.all_gather(z_part, "depth").sum(axis=0)
-    z_one = from_everyone(z_part, "cols").sum(axis=0)
+    z_one, two_old, flat, row_from, col_from, *whole = alone(
+        lambda shard: from_everyone(shard, "cols"),
+        z_part, two_old, flat, row_from, col_from, *whole,
+    )
+    z_one = z_one.sum(axis=0)
     one = mul(orth_factor(mul(z_one, z_one.T)), z_one)
 
     projected = jnp.concatenate([mul(one, matrix) for matrix in whole], axis=0)
-    projected = from_everyone(projected, "cols").reshape(-1, length_two)
+    projected, two_old, one, flat, row_from, col_from = alone(
+        lambda shard: from_everyone(shard, "cols"),
+        projected, two_old, one, flat, row_from, col_from,
+    )
+    projected = projected.reshape(-1, length_two)
     core = mul(projected, two_old)
     z_part = mul(core.T, projected)
     z_two = lax.all_gather(z_part, "depth").sum(axis=0)
     two = mul(orth_factor(mul(z_two, z_two.T)), z_two)
 
-    one_own = lax.dynamic_slice_in_dim(one, row * size_one, size_one, 1)
-    two_own = lax.dynamic_slice_in_dim(two, col * size_two, size_two, 1)
-    core = mul(two, projected.T)
+    one_own = lax.dynamic_slice_in_dim(one, row_from, size_one, 1)
+    two_own = lax.dynamic_slice_in_dim(two, col_from, size_two, 1)
     grid = projected.reshape(-1, rank_one, length_two)
     spread = jnp.einsum("ai,caj->cij", one_own, grid, precision=exact_mode)
     spread = mul(spread.reshape(-1, length_two), mul(two.T, two_own))
     spread = spread.reshape(-1, size_one * size_two)
-    core = lax.all_gather(core, "depth")
     spread = lax.all_gather(spread, "depth")
     spread = spread.reshape(depth, cols, slices, -1).transpose(1, 0, 2, 3).reshape(rank_three, -1)
     z_part = mul(spread, flat)
-    z_part = from_everyone(z_part, "cols").sum(axis=0)
+    z_part, one_own, two_own, two, projected = alone(
+        lambda shard: from_everyone(shard, "cols"), z_part, one_own, two_own, two, projected
+    )
+    z_part = z_part.sum(axis=0)
     z_three = from_everyone(z_part, "rows").sum(axis=0)
     gram = lax.all_gather(mul(z_three, z_three.T), "depth").sum(axis=0)
     three = mul(orth_factor(gram), z_three)
 
+    core = lax.all_gather(mul(two, projected.T), "depth")
     core = core.reshape(depth, rank_two, cols, slices, rank_one)
     core = core.transpose(4, 1, 2, 0, 3).reshape(rank_one, rank_two, rank_three)
     return (

time: 186 us -> 180 us (0.968)
  blocking collectives: 56.7 us -> 151 us
  starting transfers between devices: 61.6 us -> 5.79 us
  waiting for transfers between devices: 43.3 us -> 3.87 us
  between operations: 3.14 us -> 1.11 us
    all_to_all x0 -> x1, blocking collectives: none -> 51.8 us  [body(): lax.all_to_all(shard, ('cols', 'depth'), 0, 0, tiled=True)]
    all_to_all x1 -> x0, starting transfers between devices: 44.9 us -> none  [body(): got = lax.all_to_all(message, ('cols', 'depth'), 0, 0, tiled=True)]
    all_to_all x2 -> x4, blocking collectives: 31.2 us -> 74.3 us  [from_everyone(): lax.all_to_all(jnp.broadcast_to(shard[None], (peers, *shard.shape)), axis...]
    all_to_all x3 -> x1, waiting for transfers between devices: 35.4 us -> 3.87 us  [from_everyone(): lax.all_to_all(jnp.broadcast_to(shard[None], (peers, *shard.shape)), axis...]
    all_to_all x3 -> x1, starting transfers between devices: 16.8 us -> 5.79 us  [from_everyone(): lax.all_to_all(jnp.broadcast_to(shard[None], (peers, *shard.shape)), axis...]
    all_to_all x1 -> x0, waiting for transfers between devices: 7.9 us -> none  [body(): got = lax.all_to_all(message, ('cols', 'depth'), 0, 0, tiled=True)]
    dot_general x36 -> x42, matrix products: 9.84 us -> 9.46 us  [mul(): return jnp.dot(left, right, precision=exact_mode)]
  transfers between devices with their start and end apart: 4 -> 1, of which waited for: 4 -> 1; matrix products, arithmetic and copies ran while one was open for 3% -> 3% of each run, Pallas kernels for 0% -> 0%
where the time goes in v2:
time: 180 us; the launch traced here: 179 us
  blocking collectives  151 us (84%)
  matrix products  10.1 us (6%)
  local copies, waits for them, and re-layouts  7.27 us (4%)
  starting transfers between devices  5.79 us (3%)
  waiting for transfers between devices  3.87 us (2%)
    all_to_all x4, blocking collectives, from_everyone(): lax.all_to_all(jnp.broadcast_to(shard[None], (peers, *shard.shape)), axis...  74.3 us
    all_to_all x1, blocking collectives, body(): lax.all_to_all(shard, ('cols', 'depth'), 0, 0, tiled=True)  51.8 us
    dot_general x42, matrix products, mul(): return jnp.dot(left, right, precision=exact_mode)  9.46 us
    all_gather x1, blocking collectives, body(): gram = lax.all_gather(mul(z_three, z_three.T), 'depth').sum(axis=0)  8.43 us
    all_gather x1, blocking collectives, body(): z_part = lax.all_gather(z_part, 'depth').sum(axis=0)  8.08 us
    all_to_all x1, starting transfers between devices, from_everyone(): lax.all_to_all(jnp.broadcast_to(shard[None], (peers, *shard.shape)), axis...  5.79 us
    all_to_all x1, waiting for transfers between devices, from_everyone(): lax.all_to_all(jnp.broadcast_to(shard[None], (peers, *shard.shape)), axis...  3.87 us
    all_gather x1, blocking collectives, body(): core = lax.all_gather(mul(two, projected.T), 'depth')  3.75 us
  transfers between devices with their start and end apart: 1, of which 1 were waited for; matrix products, arithmetic and copies ran while one was open for 3% of the time, Pallas kernels for 0%

profile of v2, /device:TPU:65, one launch (start us, length us, event | category | flops | bytes accessed | tf_op | source)
XLA Modules:
  0.0 179.2 jit_solution(14800654652203640695)
XLA Ops:
  0.7 0.7 copy-done.2
  1.4 0.2 copy-done
  1.6 0.5 copy-done.1
  2.1 0.2 fusion.142
  2.6 51.8 %all_to_all.30 = f32[16,8,128]{2,1,0:T(8,128)S(1)} all-to-all(f32[16,8,128]{2,1,0:T(8,128)S(1)} %pad_maximum_fusion.4), channel_id=1, replica_groups=mesh['groups'=2,'rows'=16,'cols'=8,'depth'=2] {'cols','depth'}, dimensions={0} | all-to-all | bytes 131072 | tf_op jit(solution)/shard_map/all_to_all | solution.py:81
  54.8 23.1 %all_to_all.31 = f32[16,40,128]{2,1,0:T(8,128)S(1)} all-to-all(f32[16,40,128]{2,1,0:T(8,128)S(1)} %broadcast_in_dim.15), channel_id=1, replica_groups=mesh['groups'=2,'rows'=16,'cols'=8,'depth'=2] {'rows'}, dimensions={0} | all-to-all | bytes 655360 | tf_op jit(solution)/shard_map/all_to_all | solution.py:19
  78.0 0.3 fusion.144
  78.3 0.3 fusion.143
  78.6 0.4 fusion.4
  79.0 0.2 fusion.3
  79.2 8.1 %all-gather = f32[128,256]{1,0:T(8,128)S(1)} all-gather(f32[64,256]{1,0:T(8,128)S(1)} %fusion.3), channel_id=2, replica_groups=mesh['groups'=2,'rows'=16,'cols'=8,'depth'=2] {'depth'}, dimensions={0}, use_global_device_ids=true | all-gather | bytes 196608 | tf_op jit(solution)/shard_map/all_gather | solution.py:102
  87.4 20.4 %all_to_all.32 = f32[8,64,256]{2,1,0:T(8,128)S(1)} all-to-all(f32[8,64,256]{2,1,0:T(8,128)S(1)} %broadcast_in_dim.16), channel_id=1, replica_groups=mesh['groups'=2,'rows'=16,'cols'=8,'depth'=2] {'cols'}, dimensions={0} | all-to-all | bytes 1048576 | tf_op jit(solution)/shard_map/all_to_all | solution.py:19
  107.8 0.2 fusion.145
  108.0 0.2 fusion.17
  108.2 0.2 fusion.139
  108.4 0.2 fusion.16
  108.5 0.2 fusion.15
  108.7 0.2 fusion.14
  108.9 0.2 fusion.13
  109.0 0.2 fusion.1
  109.2 0.2 convolution_multiply_fusion.2
  109.4 0.2 fusion.146
  109.6 0.2 fusion.148
  109.8 0.2 fusion.147
  110.1 19.9 %all_to_all.33 = f32[8,128,128]{2,1,0:T(8,128)S(1)} all-to-all(f32[8,128,128]{2,1,0:T(8,128)S(1)} %broadcast_in_dim.17), channel_id=1, replica_groups=mesh['groups'=2,'rows'=16,'cols'=8,'depth'=2] {'cols'}, dimensions={0} | all-to-all | bytes 1048576 | tf_op jit(solution)/shard_map/all_to_all | solution.py:19
  130.0 0.7 fusion.149
  130.7 0.4 fusion.150
  131.1 2.6 %all-gather.1 = f32[128,128]{1,0:T(8,128)S(1)} all-gather(f32[64,128]{1,0:T(8,128)S(1)} %fusion.150), channel_id=3, replica_groups=mesh['groups'=2,'rows'=16,'cols'=8,'depth'=2] {'depth'}, dimensions={0}, use_global_device_ids=true | all-gather | bytes 98304 | tf_op jit(solution)/shard_map/all_gather | solution.py:118
  133.7 0.2 fusion.151
  133.9 0.2 fusion.11
  134.1 0.2 fusion.140
  134.2 0.2 fusion.10
  134.4 0.2 fusion.9
  134.6 0.2 fusion.8
  134.7 0.2 fusion.7
  134.9 0.2 fusion
  135.1 0.2 convolution_multiply_fusion
  135.3 0.2 fusion.152
  135.5 0.2 fusion.153
  135.8 0.4 fusion.5
  136.2 0.2 fusion.154
  136.6 1.9 %all_gather.31 = f32[2,16,256]{2,1,0:T(8,128)S(1)} all-gather(f32[1,16,256]{2,1,0:T(8,128)S(1)} %all_gather_reshape.3), channel_id=1, replica_groups=mesh['groups'=2,'rows'=16,'cols'=8,'depth'=2] {'depth'}, dimensions={0}, use_global_device_ids=true | all-gather | bytes 49152 | tf_op jit(solution)/shard_map/all_gather | solution.py:127
  138.5 0.2 fusion.155
  138.8 10.8 %all_to_all.34 = f32[8,32,128]{2,1,0:T(8,128)S(1)} all-to-all(f32[8,32,128]{2,1,0:T(8,128)S(1)} %broadcast_in_dim.18), channel_id=1, replica_groups=mesh['groups'=2,'rows'=16,'cols'=8,'depth'=2] {'cols'}, dimensions={0} | all-to-all | bytes 262144 | tf_op jit(solution)/shard_map/all_to_all | solution.py:19
  149.6 0.7 broadcast_in_dim.19
  150.3 5.8 %all-to-all-start.5 = ((f32[16,32,128]{2,1,0:T(8,128)}), f32[16,32,128]{2,1,0:T(8,128)S(1)}, u32[]{:S(2)}, u32[]{:S(2)}) async-start(f32[16,32,128]{2,1,0:T(8,128)} %broadcast_in_dim.19), calls=%async_computation.5 | async-start | bytes 524288 | tf_op jit(solution)/shard_map/all_to_all | solution.py:19
  156.2 0.7 copy.43
  156.8 0.7 copy.42
  157.5 0.7 fusion.157
  158.2 3.8 %all-gather.3 = f32[128,1024]{1,0:T(8,128)S(1)} all-gather(f32[64,1024]{1,0:T(8,128)S(1)} %fusion.157), channel_id=5, replica_groups=mesh['groups'=2,'rows'=16,'cols'=8,'depth'=2] {'depth'}, dimensions={0}, use_global_device_ids=true | all-gather | bytes 786432 | tf_op jit(solution)/shard_map/all_gather | solution.py:138
  161.9 0.8 reshape.76
  162.7 2.1 %copy.41 = f32[64,64,8,2,2]{1,4,3,2,0:T(2,128)} copy(f32[64,64,8,2,2]{0,4,2,1,3:T(2,128)S(1)} %bitcast.105) | data formatting | bytes 1048576 | tf_op jit(solution)/shard_map/transpose | solution.py:140
  164.8 3.9 %all-to-all-done.5 = f32[16,32,128]{2,1,0:T(8,128)S(1)} async-done(((f32[16,32,128]{2,1,0:T(8,128)}), f32[16,32,128]{2,1,0:T(8,128)S(1)}, u32[]{:S(2)}, u32[]{:S(2)}) %all-to-all-start.5) | async-done | bytes 262176 | tf_op jit(solution)/shard_map/all_to_all | solution.py:19
  168.7 0.1 fusion.156
  168.8 8.4 %all-gather.2 = f32[64,32]{1,0:T(8,128)S(1)} all-gather(f32[32,32]{1,0:T(8,128)S(1)} %fusion.156), channel_id=4, replica_groups=mesh['groups'=2,'rows'=16,'cols'=8,'depth'=2] {'depth'}, dimensions={0}, use_global_device_ids=true | all-gather | bytes 12288 | tf_op jit(solution)/shard_map/all_gather | solution.py:135
  177.3 0.1 fusion.23
  177.4 0.2 fusion.141
  177.6 0.1 fusion.22
  177.7 0.2 fusion.21
  177.9 0.1 fusion.20
  178.0 0.2 fusion.19
  178.2 0.2 fusion.2
  178.3 0.1 convolution_multiply_fusion.5
  178.5 0.8 convolution_multiply_fusion.4
  (41 shorter events, 1.3 us)
Async XLA Ops:
  0.6 0.9 copy-start
  0.7 0.7 copy-start.2
  0.7 0.7 copy-start.3
  1.4 0.7 copy-start.1
  150.3 18.3 %all-to-all-start.5 = ((f32[16,32,128]{2,1,0:T(8,128)}), f32[16,32,128]{2,1,0:T(8,128)S(1)}, u32[]{:S(2)}, u32[]{:S(2)}) async-start(f32[16,32,128]{2,1,0:T(8,128)} %broadcast_in_dim.19), calls=%async_computation.5 | async-start | bytes 524288 | tf_op jit(solution)/shard_map/all_to_all | solution.py:19

commit v3 on v2

--- a/solution.py
+++ b/solution.py
@@ -7,6 +7,7 @@
 
 NEWTON = 3
 LANES = 128
+CLASSES = 4
 exact_mode = lax.Precision.HIGHEST
 
 
@@ -58,23 +59,23 @@
     rank_two = start_two.shape[1]
     rank_three = start_three.shape[1]
     rows, cols, depth = (lax.axis_size(name) for name in ("rows", "cols", "depth"))
-    level = lax.axis_index("depth")
     row_from = lax.axis_index("rows") * size_one
     col_from = lax.axis_index("cols") * size_two
     length_one, length_two, length_three = size_one * rows, size_two * cols, size_three * depth
-    owners = cols * depth
-    slices = rank_three // owners
+    teams = [list(range(first, first + CLASSES)) for first in range(0, cols, CLASSES)]
+    slices = rank_three // (CLASSES * depth)
     flat = tensor.reshape(size_one * size_two, size_three)
 
     thinned = lax.dot_general(
         start_three, flat, (((0,), (1,)), ((), ())), precision=exact_mode
-    ).reshape(owners, -1, LANES)
+    ).reshape(1, depth, CLASSES, -1, LANES)
+    lines = thinned.shape[3]
     two_packed = halves_side_by_side(start_two)
-    part = two_packed.shape[0] // depth
-    two_part = lax.dynamic_slice_in_dim(two_packed, level * part, part, 0)
-    lines = thinned.shape[1]
+    thinned = jnp.broadcast_to(
+        thinned.transpose(0, 2, 1, 3, 4), (len(teams), CLASSES, depth, lines, LANES)
+    ).reshape(cols * depth, lines, LANES)
     message = jnp.concatenate(
-        [thinned, jnp.broadcast_to(two_part[None], (owners, *two_part.shape))], axis=1
+        [thinned, jnp.broadcast_to(two_packed[None], (cols * depth, *two_packed.shape))], axis=1
     )
     one_packed = halves_side_by_side(start_one)
     got, one_packed, flat, row_from, col_from = alone(
@@ -84,11 +85,11 @@
     got = got.reshape(cols, depth, *got.shape[1:])
     own = got[:, :, :lines].sum(axis=1).reshape(cols, slices * size_one, size_two)
     own = own.transpose(1, 0, 2).reshape(slices * size_one, length_two)
-    two_old = halves_stacked(got[:, :, lines:].reshape(cols, depth * part, 2 * rank_two))
+    two_old = halves_stacked(got[:, 0, lines:])
 
-    message = jnp.concatenate([own, one_packed], axis=0)
     got, two_old, flat, row_from, col_from = alone(
-        lambda shard: from_everyone(shard, "rows"), message, two_old, flat, row_from, col_from
+        lambda shard: lax.all_gather(shard, "rows"),
+        jnp.concatenate([own, one_packed], axis=0), two_old, flat, row_from, col_from,
     )
     whole = [
         got[:, c * size_one : (c + 1) * size_one].reshape(length_one, length_two)
@@ -100,18 +101,11 @@
     core = mul(one_old.T, unfolded)
     z_part = mul(core, unfolded.T)
     z_part = lax.all_gather(z_part, "depth").sum(axis=0)
-    z_one, two_old, flat, row_from, col_from, *whole = alone(
-        lambda shard: from_everyone(shard, "cols"),
-        z_part, two_old, flat, row_from, col_from, *whole,
-    )
-    z_one = z_one.sum(axis=0)
+    z_one = lax.all_gather(z_part, "cols", axis_index_groups=teams).sum(axis=0)
     one = mul(orth_factor(mul(z_one, z_one.T)), z_one)
 
     projected = jnp.concatenate([mul(one, matrix) for matrix in whole], axis=0)
-    projected, two_old, one, flat, row_from, col_from = alone(
-        lambda shard: from_everyone(shard, "cols"),
-        projected, two_old, one, flat, row_from, col_from,
-    )
+    projected = lax.all_gather(projected, "cols", axis_index_groups=teams)
     projected = projected.reshape(-1, length_two)
     core = mul(projected, two_old)
     z_part = mul(core.T, projected)
@@ -124,8 +118,7 @@
     spread = jnp.einsum("ai,caj->cij", one_own, grid, precision=exact_mode)
     spread = mul(spread.reshape(-1, length_two), mul(two.T, two_own))
     spread = spread.reshape(-1, size_one * size_two)
-    spread = lax.all_gather(spread, "depth")
-    spread = spread.reshape(depth, cols, slices, -1).transpose(1, 0, 2, 3).reshape(rank_three, -1)
+    spread = lax.all_gather(spread, "depth", axis=0, tiled=True)
     z_part = mul(spread, flat)
     z_part, one_own, two_own, two, projected = alone(
         lambda shard: from_everyone(shard, "cols"), z_part, one_own, two_own, two, projected
@@ -136,8 +129,8 @@
     three = mul(orth_factor(gram), z_three)
 
     core = lax.all_gather(mul(two, projected.T), "depth")
-    core = core.reshape(depth, rank_two, cols, slices, rank_one)
-    core = core.transpose(4, 1, 2, 0, 3).reshape(rank_one, rank_two, rank_three)
+    core = core.reshape(depth, rank_two, -1, rank_one)
+    core = core.transpose(3, 1, 0, 2).reshape(rank_one, rank_two, rank_three)
     return (
         one_own.T * math.sqrt(length_one),
         two_own.T * math.sqrt(length_two),

time: 180 us -> 174 us (0.967)
  blocking collectives: 151 us -> 147 us
  starting transfers between devices: 5.79 us -> 3.97 us
    all_to_all x4 -> x1, blocking collectives: 74.3 us -> 11.3 us  [from_everyone(): lax.all_to_all(jnp.broadcast_to(shard[None], (peers, *shard.shape)), axis...]
    all_gather x1 -> x4, blocking collectives: 1.88 us -> 55.4 us  [the longest x1 28.6 us: body(): lax.all_gather(shard, 'rows')]
    all_gather x1, blocking collectives: 2.56 us -> 5.93 us  [body(): z_two = lax.all_gather(z_part, 'depth').sum(axis=0)]
    all_to_all x1, starting transfers between devices: 5.79 us -> 3.97 us  [from_everyone(): lax.all_to_all(jnp.broadcast_to(shard[None], (peers, *shard.shape)), axis...]
    dot_general x42 -> x46, matrix products: 9.46 us -> 10.5 us  [mul(): return jnp.dot(left, right, precision=exact_mode)]
  transfers between devices with their start and end apart: 1 -> 1, of which waited for: 1 -> 1; matrix products, arithmetic and copies ran while one was open for 3% -> 2% of each run, Pallas kernels for 0% -> 0%
where the time goes in v3:
time: 174 us
  blocking collectives  147 us (84%)
  matrix products  11.2 us (6%)
  local copies, waits for them, and re-layouts  6.58 us (4%)
  waiting for transfers between devices  4.23 us (2%)
  starting transfers between devices  3.97 us (2%)
    all_to_all x1, blocking collectives, body(): lax.all_to_all(shard, ('cols', 'depth'), 0, 0, tiled=True)  53.1 us
    all_gather x1, blocking collectives, body(): lax.all_gather(shard, 'rows')  28.6 us
    all_gather x1, blocking collectives, body(): projected = lax.all_gather(projected, 'cols', axis_index_groups=teams)  13.7 us
    all_to_all x1, blocking collectives, from_everyone(): lax.all_to_all(jnp.broadcast_to(shard[None], (peers, *shard.shape)), axis...  11.3 us
    all_gather x1, blocking collectives, body(): z_one = lax.all_gather(z_part, 'cols', axis_index_groups=teams).sum(axis=0)  11.2 us
    dot_general x46, matrix products, mul(): return jnp.dot(left, right, precision=exact_mode)  10.5 us
    all_gather x1, blocking collectives, body(): z_part = lax.all_gather(z_part, 'depth').sum(axis=0)  8.71 us
    all_gather x1, blocking collectives, body(): gram = lax.all_gather(mul(z_three, z_three.T), 'depth').sum(axis=0)  8.14 us
  transfers between devices with their start and end apart: 1, of which 1 were waited for; matrix products, arithmetic and copies ran while one was open for 2% of the time, Pallas kernels for 0%

profile of v3, /device:TPU:65, one launch (start us, length us, event | category | flops | bytes accessed | tf_op | source)
XLA Modules:
  0.0 174.0 jit_solution(12680599170066680902)
XLA Ops:
  0.7 0.7 copy-done.2
  1.4 0.2 copy-done
  1.6 0.5 copy-done.1
  2.1 0.2 fusion.141
  2.6 53.1 %all_to_all.15 = f32[16,16,128]{2,1,0:T(8,128)S(1)} all-to-all(f32[16,16,128]{2,1,0:T(8,128)S(1)} %pad_maximum_fusion.3), channel_id=1, replica_groups=mesh['groups'=2,'rows'=16,'cols'=8,'depth'=2] {'cols','depth'}, dimensions={0} | all-to-all | bytes 262144 | tf_op jit(solution)/shard_map/all_to_all | solution.py:82
  56.3 28.6 %all-gather = f32[1152,128]{1,0:T(8,128)S(1)} all-gather(f32[72,128]{1,0:T(8,128)S(1)} %copy.52), channel_id=2, replica_groups=mesh['groups'=2,'rows'=16,'cols'=8,'depth'=2] {'rows'}, dimensions={0}, use_global_device_ids=true | all-gather | bytes 626688 | tf_op jit(solution)/shard_map/all_gather | solution.py:91
  85.1 0.3 fusion.145
  85.4 0.3 fusion.142
  85.7 0.3 fusion.144
  86.0 0.3 fusion.143
  86.3 0.4 fusion.4
  86.7 0.2 fusion.3
  86.9 8.7 %all-gather.1 = f32[128,256]{1,0:T(8,128)S(1)} all-gather(f32[64,256]{1,0:T(8,128)S(1)} %fusion.3), channel_id=3, replica_groups=mesh['groups'=2,'rows'=16,'cols'=8,'depth'=2] {'depth'}, dimensions={0}, use_global_device_ids=true | all-gather | bytes 196608 | tf_op jit(solution)/shard_map/all_gather | solution.py:103
  95.7 11.2 %all-gather.2 = f32[256,256]{1,0:T(8,128)S(1)} all-gather(f32[64,256]{1,0:T(8,128)S(1)} %reduce_sum.64), channel_id=4, replica_groups={{0,2,4,6},{8,10,12,14},{1,3,5,7},{9,11,13,15},{16,18,20,22},{24,26,28,3..., dimensions={0}, use_global_device_ids=true | all-gather | bytes 327680 | tf_op jit(solution)/shard_map/all_gather | solution.py:104
  106.9 0.2 fusion.146
  107.1 0.2 fusion.17
  107.2 0.2 fusion.138
  107.4 0.2 fusion.16
  107.6 0.2 fusion.15
  107.8 0.2 fusion.14
  107.9 0.2 fusion.13
  108.1 0.2 fusion.1
  108.3 0.2 convolution_multiply_fusion.2
  108.5 0.2 fusion.147
  108.7 0.2 fusion.151
  108.9 0.2 fusion.150
  109.1 0.2 fusion.149
  109.3 0.2 fusion.148
  109.6 13.7 %all-gather.3 = f32[1024,128]{1,0:T(8,128)S(1)} all-gather(f32[256,128]{1,0:T(8,128)S(1)} %pad_maximum_fusion.5), channel_id=5, replica_groups={{0,2,4,6},{8,10,12,14},{1,3,5,7},{9,11,13,15},{16,18,20,22},{24,26,28,3..., dimensions={0}, use_global_device_ids=true | all-gather | bytes 655360 | tf_op jit(solution)/shard_map/all_gather | solution.py:108
  123.3 0.7 fusion.152
  124.0 0.4 fusion.153
  124.4 5.9 %all-gather.4 = f32[128,128]{1,0:T(8,128)S(1)} all-gather(f32[64,128]{1,0:T(8,128)S(1)} %fusion.153), channel_id=6, replica_groups=mesh['groups'=2,'rows'=16,'cols'=8,'depth'=2] {'depth'}, dimensions={0}, use_global_device_ids=true | all-gather | bytes 98304 | tf_op jit(solution)/shard_map/all_gather | solution.py:112
  130.4 0.2 fusion.154
  130.6 0.2 fusion.11
  130.7 0.2 fusion.139
  130.9 0.2 fusion.10
  131.1 0.2 fusion.9
  131.3 0.2 fusion.8
  131.4 0.2 fusion.7
  131.7 0.2 fusion
  131.9 0.2 convolution_multiply_fusion
  132.0 0.2 fusion.155
  132.3 0.2 fusion.156
  132.5 0.4 fusion.5
  132.9 0.2 fusion.157
  133.3 1.9 %all_gather.55 = f32[32,256]{1,0:T(8,128)S(1)} all-gather(f32[16,256]{1,0:T(8,128)S(1)} %reshape.76), channel_id=1, replica_groups=mesh['groups'=2,'rows'=16,'cols'=8,'depth'=2] {'depth'}, dimensions={0}, use_global_device_ids=true | all-gather | bytes 49152 | tf_op jit(solution)/shard_map/all_gather | solution.py:121
  135.2 0.2 fusion.158
  135.4 11.3 %all_to_all.16 = f32[8,32,128]{2,1,0:T(8,128)S(1)} all-to-all(f32[8,32,128]{2,1,0:T(8,128)S(1)} %broadcast_in_dim.15), channel_id=1, replica_groups=mesh['groups'=2,'rows'=16,'cols'=8,'depth'=2] {'cols'}, dimensions={0} | all-to-all | bytes 262144 | tf_op jit(solution)/shard_map/all_to_all | solution.py:20
  146.7 0.7 broadcast_in_dim.32
  147.4 4.0 %all-to-all-start.2 = ((f32[16,32,128]{2,1,0:T(8,128)}), f32[16,32,128]{2,1,0:T(8,128)S(1)}, u32[]{:S(2)}, u32[]{:S(2)}) async-start(f32[16,32,128]{2,1,0:T(8,128)} %broadcast_in_dim.32), calls=%async_computation.2 | async-start | bytes 524288 | tf_op jit(solution)/shard_map/all_to_all | solution.py:20
  151.4 0.7 copy.58
  152.1 0.7 copy.57
  152.7 0.7 fusion.160
  153.4 3.9 %all-gather.6 = f32[128,1024]{1,0:T(8,128)S(1)} all-gather(f32[64,1024]{1,0:T(8,128)S(1)} %fusion.160), channel_id=8, replica_groups=mesh['groups'=2,'rows'=16,'cols'=8,'depth'=2] {'depth'}, dimensions={0}, use_global_device_ids=true | all-gather | bytes 786432 | tf_op jit(solution)/shard_map/all_gather | solution.py:131
  157.3 0.3 reshape.77
  157.6 1.9 %copy.56 = f32[64,64,2,16]{1,3,2,0:T(8,128)} copy(f32[64,64,2,16]{0,3,1,2:T(8,128)S(1)} %bitcast.111) | data formatting | bytes 1048576 | tf_op jit(solution)/shard_map/transpose | solution.py:133
  159.5 4.2 %all-to-all-done.2 = f32[16,32,128]{2,1,0:T(8,128)S(1)} async-done(((f32[16,32,128]{2,1,0:T(8,128)}), f32[16,32,128]{2,1,0:T(8,128)S(1)}, u32[]{:S(2)}, u32[]{:S(2)}) %all-to-all-start.2) | async-done | bytes 262176 | tf_op jit(solution)/shard_map/all_to_all | solution.py:20
  163.7 0.1 fusion.159
  163.9 8.1 %all-gather.5 = f32[64,32]{1,0:T(8,128)S(1)} all-gather(f32[32,32]{1,0:T(8,128)S(1)} %fusion.159), channel_id=7, replica_groups=mesh['groups'=2,'rows'=16,'cols'=8,'depth'=2] {'depth'}, dimensions={0}, use_global_device_ids=true | all-gather | bytes 12288 | tf_op jit(solution)/shard_map/all_gather | solution.py:128
  172.2 0.2 fusion.140
  172.5 0.2 fusion.21
  172.8 0.2 fusion.19
  172.9 0.2 fusion.2
  173.2 0.8 convolution_multiply_fusion.4
  (44 shorter events, 1.9 us)
Async XLA Ops:
  0.6 0.9 copy-start
  0.6 0.7 copy-start.2
  0.7 0.7 copy-start.3
  1.4 0.7 copy-start.1
  147.4 16.3 %all-to-all-start.2 = ((f32[16,32,128]{2,1,0:T(8,128)}), f32[16,32,128]{2,1,0:T(8,128)S(1)}, u32[]{:S(2)}, u32[]{:S(2)}) async-start(f32[16,32,128]{2,1,0:T(8,128)} %broadcast_in_dim.32), calls=%async_computation.2 | async-start | bytes 524288 | tf_op jit(solution)/shard_map/all_to_all | solution.py:20

commit v4 on v3

v4 whole, which is shorter than its diff:
```python
import functools
import math

import jax
import jax.numpy as jnp
from jax import lax
from jax.experimental import pallas as pl
from jax.experimental.pallas import tpu as pltpu
from jax.sharding import PartitionSpec as P

NEWTON = 3
LANES = 128
CLASSES = 4
KERNEL_BYTES = 8 * 2**20
exact_mode = lax.Precision.HIGHEST


def mul(left, right):
    return jnp.dot(left, right, precision=exact_mode)


def from_everyone(shard, axis):
    peers = lax.axis_size(axis)
    return lax.all_to_all(
        jnp.broadcast_to(shard[None], (peers, *shard.shape)), axis, 0, 0, tiled=True
    )


def alone(operation, shard, *others):
    shard, others = lax.optimization_barrier((shard, others))
    return lax.optimization_barrier((operation(shard), *others))


def mul_nt(left, right):
    return lax.dot_general(left, right, (((1,), (1,)), ((), ())), precision=exact_mode)


def mul_tn(left, right):
    return lax.dot_general(left, right, (((0,), (0,)), ((), ())), precision=exact_mode)


def orth_factor(gram):
    down = lax.broadcasted_iota(jnp.int32, gram.shape, 0)
    across = lax.broadcasted_iota(jnp.int32, gram.shape, 1)
    identity = (down == across).astype(jnp.float32)
    total = jnp.sum(gram * identity, keepdims=True) + 1e-06
    gram = gram / total
    factor = None
    for step in range(NEWTON):
        move = 1.5 * identity - 0.5 * gram
        factor = move if factor is None else mul(factor, move)
        if step + 1 < NEWTON:
            gram = mul(mul(move, gram), move)
    return factor / jnp.sqrt(total)


def kernel_call(kernel, shapes, *operands):
    one = not isinstance(shapes[0], tuple)
    whole = pl.BlockSpec(memory_space=pltpu.VMEM)
    outs = [jax.ShapeDtypeStruct(shape, jnp.float32) for shape in ([shapes] if one else shapes)]
    return pl.pallas_call(
        kernel,
        out_shape=outs[0] if one else outs,
        in_specs=[whole] * len(operands),
        out_specs=whole if one else [whole] * len(outs),
        compiler_params=pltpu.CompilerParams(vmem_limit_bytes=KERNEL_BYTES),
    )(*operands)


def first_mode(size_one, slices, got, two_old, z_part):
    packed = got[:, slices * size_one :, :]
    width = packed.shape[2] // 2
    one_old = jnp.stack([packed[:, :, :width], packed[:, :, width:]], axis=1)
    one_old = one_old.reshape(-1, width)
    two = two_old[...]
    total = None
    for c in range(slices):
        matrix = got[:, c * size_one : (c + 1) * size_one, :].reshape(-1, two.shape[0])
        unfolded = mul(matrix, two)
        term = mul_nt(mul_tn(one_old, unfolded), unfolded)
        total = term if total is None else total + term
    z_part[...] = total


def to_second(size_one, slices, z_parts, got, one, projected):
    z = jnp.sum(z_parts[...], axis=0)
    new = mul(orth_factor(mul_nt(z, z)), z)
    one[...] = new
    rank = new.shape[0]
    for c in range(slices):
        matrix = got[:, c * size_one : (c + 1) * size_one, :].reshape(new.shape[1], -1)
        projected[c * rank : (c + 1) * rank, :] = mul(new, matrix)


def second_mode(projected, two_old, z_part):
    z_part[...] = mul_tn(mul(projected[...], two_old[...]), projected[...])


def to_third(z_parts, projected, one, one_pick, two_pick, two, one_own, two_own, spread):
    z = jnp.sum(z_parts[...], axis=0)
    new = mul(orth_factor(mul_nt(z, z)), z)
    two[...] = new
    first = mul_nt(one_pick[...], one[...])
    second = mul_nt(two_pick[...], new)
    one_own[...] = first * math.sqrt(one.shape[1])
    two_own[...] = second * math.sqrt(new.shape[1])
    joined = mul(second, new)
    rank = first.shape[1]
    for c in range(projected.shape[0] // rank):
        grid = mul(first, projected[c * rank : (c + 1) * rank, :])
        spread[c * first.shape[0] : (c + 1) * first.shape[0], :] = mul_nt(grid, joined)


def last_orth(scale, grams, z, three):
    factor = orth_factor(jnp.sum(grams[...], axis=0))
    three[...] = mul_tn(z[...], factor) * scale


def own_rows(axis, size, length):
    down = lax.broadcasted_iota(jnp.int32, (size, length), 0)
    across = lax.broadcasted_iota(jnp.int32, (size, length), 1)
    return (across == down + lax.axis_index(axis) * size).astype(jnp.float32)


def halves_side_by_side(block):
    half = block.shape[0] // 2
    return jnp.concatenate([block[:half], block[half:]], axis=1)


def halves_stacked(blocks):
    count, half, width = blocks.shape
    width //= 2
    pairs = jnp.stack([blocks[:, :, :width], blocks[:, :, width:]], axis=1)
    return pairs.reshape(count * 2 * half, width)


def body(tensor, start_one, start_two, start_three):
    size_one, size_two, size_three = tensor.shape
    rank_one = start_one.shape[1]
    rank_two = start_two.shape[1]
    rank_three = start_three.shape[1]
    rows, cols, depth = (lax.axis_size(name) for name in ("rows", "cols", "depth"))
    length_one, length_two, length_three = size_one * rows, size_two * cols, size_three * depth
    one_pick = own_rows("rows", size_one, length_one)
    two_pick = own_rows("cols", size_two, length_two)
    teams = [list(range(first, first + CLASSES)) for first in range(0, cols, CLASSES)]
    half_team = CLASSES // 2
    near = [
        list(range(first * depth, (first + half_team) * depth))
        for first in range(0, cols, half_team)
    ]
    far = [
        [first + at, first + half_team + at]
        for first in range(0, cols, CLASSES)
        for at in range(half_team)
    ]
    slices = rank_three // (CLASSES * depth)
    flat = tensor.reshape(size_one * size_two, size_three)

    thinned = lax.dot_general(
        start_three, flat, (((0,), (1,)), ((), ())), precision=exact_mode
    ).reshape(1, depth, CLASSES, -1, LANES)
    lines = thinned.shape[3]
    two_packed = halves_side_by_side(start_two)
    thinned = jnp.broadcast_to(
        thinned.transpose(0, 2, 1, 3, 4), (len(teams), CLASSES, depth, lines, LANES)
    ).reshape(cols * depth, lines, LANES)
    message = jnp.concatenate(
        [thinned, jnp.broadcast_to(two_packed[None], (cols * depth, *two_packed.shape))], axis=1
    )
    one_packed = halves_side_by_side(start_one)
    got, one_packed, flat, one_pick, two_pick = alone(
        lambda shard: lax.all_to_all(shard, ("cols", "depth"), 0, 0, tiled=True),
        message, one_packed, flat, one_pick, two_pick,
    )
    got = got.reshape(cols, depth, *got.shape[1:])
    own = got[:, :, :lines].sum(axis=1).reshape(cols, slices * size_one, size_two)
    own = own.transpose(1, 0, 2).reshape(slices * size_one, length_two)
    two_old = halves_stacked(got[:, 0, lines:])

    got = lax.all_gather(jnp.concatenate([own, one_packed], axis=0), "rows")

    cut = (size_one, slices)
    z_part = kernel_call(
        functools.partial(first_mode, *cut), (rank_one, length_one), got, two_old
    )
    z_part = lax.all_gather(z_part, ("cols", "depth"), axis_index_groups=near).sum(axis=0)
    z_parts = lax.all_gather(z_part, "cols", axis_index_groups=far)

    one, projected = kernel_call(
        functools.partial(to_second, *cut),
        ((rank_one, length_one), (slices * rank_one, length_two)),
        z_parts,
        got,
    )
    projected = lax.all_gather(projected, "cols", axis_index_groups=teams)
    projected = projected.reshape(-1, length_two)
    z_part = kernel_call(second_mode, (rank_two, length_two), projected, two_old)
    z_parts = lax.all_gather(z_part, "depth")

    half = projected.shape[0] // rank_one
    two, one_own, two_own, spread = kernel_call(
        to_third,
        (
            (rank_two, length_two),
            (size_one, rank_one),
            (size_two, rank_two),
            (half * size_one, size_two),
        ),
        z_parts,
        projected,
        one,
        one_pick,
        two_pick,
    )
    spread = lax.all_gather(spread.reshape(half, -1), "depth", axis=0, tiled=True)
    z_part = mul(spread, flat)
    z_part, two, projected, one_own, two_own = alone(
        lambda shard: from_everyone(shard, "cols"), z_part, two, projected, one_own, two_own
    )
    z_part = z_part.sum(axis=0)
    z_three = from_everyone(z_part, "rows").sum(axis=0)
    grams = lax.all_gather(mul(z_three, z_three.T), "depth")
    three = kernel_call(
        functools.partial(last_orth, math.sqrt(length_three)),
        (size_three, rank_three),
        grams,
        z_three,
    )

    core = lax.all_gather(mul(two, projected.T), "depth")
    core = core.reshape(depth, rank_two, -1, rank_one)
    core = core.transpose(3, 1, 0, 2).reshape(rank_one, rank_two, rank_three)
    return one_own, two_own, three, core


def solution(mesh):
    in_specs = (
        P(("groups", "rows"), "cols", "depth"),
        P(("groups", "rows"), None),
        P(("groups", "cols"), None),
        P(("groups", "depth"), None),
    )
    out_specs = (
        P(("groups", "rows"), None),
        P(("groups", "cols"), None),
        P(("groups", "depth"), None),
        P("groups", None, None),
    )
    return jax.shard_map(body, mesh=mesh, in_specs=in_specs, out_specs=out_specs, check_vma=False)
```

time: 174 us -> 175 us (level)
  Pallas kernels: 0 us -> 11.1 us
  matrix products: 11.2 us -> 1.22 us
  blocking collectives: 147 us -> 145 us
  waiting for transfers between devices: 4.23 us -> 6.05 us
    pallas_call x0 -> x5, Pallas kernels: none -> 11.1 us  [kernel_call(): pl.pallas_call(kernel, out_shape=outs[0] if one else outs, in_specs=[whol...]
    dot_general x46 -> x3, matrix products: 10.5 us -> 0.99 us  [mul(): return jnp.dot(left, right, precision=exact_mode)]
    all_to_all x1, waiting for transfers between devices: 4.23 us -> 6.05 us  [from_everyone(): lax.all_to_all(jnp.broadcast_to(shard[None], (peers, *shard.shape)), axis...]
where the time goes in v4:
time: 175 us; the launch traced here: 174 us
  blocking collectives  145 us (83%)
  Pallas kernels  11.1 us (6%)
  local copies, waits for them, and re-layouts  6.16 us (4%)
  waiting for transfers between devices  6.05 us (3%)
  starting transfers between devices  3.97 us (2%)
    all_to_all x1, blocking collectives, body(): lax.all_to_all(shard, ('cols', 'depth'), 0, 0, tiled=True)  53.1 us
    all_gather x1, blocking collectives, body(): got = lax.all_gather(jnp.concatenate([own, one_packed], axis=0), 'rows')  28.6 us
    all_gather x1, blocking collectives, body(): lax.all_gather(z_part, ('cols', 'depth'), axis_index_groups=near)  12.8 us
    all_gather x1, blocking collectives, body(): projected = lax.all_gather(projected, 'cols', axis_index_groups=teams)  12.2 us
    pallas_call x5, Pallas kernels, kernel_call(): pl.pallas_call(kernel, out_shape=outs[0] if one else outs, in_specs=[whol...  11.1 us
    all_to_all x1, blocking collectives, from_everyone(): lax.all_to_all(jnp.broadcast_to(shard[None], (peers, *shard.shape)), axis...  10.8 us
    all_gather x1, blocking collectives, body(): grams = lax.all_gather(mul(z_three, z_three.T), 'depth')  8.39 us
    all_gather x1, blocking collectives, body(): z_parts = lax.all_gather(z_part, 'cols', axis_index_groups=far)  7.03 us
  transfers between devices with their start and end apart: 1, of which 1 were waited for; matrix products, arithmetic and copies ran while one was open for 2% of the time, Pallas kernels for 0%

profile of v4, /device:TPU:65, one launch (start us, length us, event | category | flops | bytes accessed | tf_op | source)
XLA Modules:
  0.0 174.3 jit_solution(10664525461299222194)
XLA Ops:
  0.6 0.0 copy-start
  0.7 0.0 copy-start.2
  0.7 0.1 fusion.1.two_pick
  0.8 0.6 copy-done.2
  1.4 0.0 copy-start.3
  1.4 0.7 copy-done.3
  2.1 0.0 copy-start.1
  2.1 0.1 fusion.one_pick
  2.2 0.0 copy-done
  2.2 0.6 copy-done.1
  2.8 0.2 fusion.4
  3.1 0.1 pad_maximum_fusion.4
  3.1 0.1 pad_maximum_fusion.3
  3.3 53.1 %all_to_all.15 = f32[16,16,128]{2,1,0:T(8,128)S(1)} all-to-all(f32[16,16,128]{2,1,0:T(8,128)S(1)} %pad_maximum_fusion), channel_id=1, replica_groups=mesh['groups'=2,'rows'=16,'cols'=8,'depth'=2] {'cols','depth'}, dimensions={0} | all-to-all | bytes 262144 | tf_op jit(solution)/shard_map/all_to_all | solution.py:173
  56.4 0.1 slice_bitcast_fusion.1
  56.5 0.1 copy.29
  56.6 0.1 reshape.48
  56.7 0.1 copy.28
  56.8 0.1 pad_maximum_fusion.1
  56.9 0.1 copy.30
  57.0 28.6 %all-gather = f32[1152,128]{1,0:T(8,128)S(1)} all-gather(f32[72,128]{1,0:T(8,128)S(1)} %copy.30), channel_id=2, replica_groups=mesh['groups'=2,'rows'=16,'cols'=8,'depth'=2] {'rows'}, dimensions={0}, use_global_device_ids=true | all-gather | bytes 626688 | tf_op jit(solution)/shard_map/all_gather | solution.py:181
  85.6 2.1 %shard_map.75 = f32[64,256]{1,0:T(8,128)S(1)} custom-call(f32[16,72,128]{2,1,0:T(8,128)S(1)} %bitcast.32, f32[128,64]{1,0:T(8,128)S(1)} %bitcast.34), custom_call_target="tpu_custom_call" | custom-call | tf_op jit(solution)/shard_map/pallas_call | solution.py:61
  87.8 12.8 %all-gather.1 = f32[256,256]{1,0:T(8,128)S(1)} all-gather(f32[64,256]{1,0:T(8,128)S(1)} %shard_map.75), channel_id=3, replica_groups={{0,1,2,3},{4,5,6,7},{8,9,10,11},{12,13,14,15},{16,17,18,19},{20,21,22,2..., dimensions={0}, use_global_device_ids=true | all-gather | bytes 327680 | tf_op jit(solution)/shard_map/all_gather | solution.py:187
  100.6 7.0 %all-gather.2 = f32[128,256]{1,0:T(8,128)S(1)} all-gather(f32[64,256]{1,0:T(8,128)S(1)} %reduce_sum.37), channel_id=4, replica_groups={{0,4},{2,6},{8,12},{10,14},{1,5},{3,7},{9,13},{11,15},{16,20},{18,22},{..., dimensions={0}, use_global_device_ids=true | all-gather | bytes 196608 | tf_op jit(solution)/shard_map/all_gather | solution.py:188
  107.6 1.8 %shard_map.76 = (f32[64,256]{1,0:T(8,128)S(1)}, f32[256,128]{1,0:T(8,128)S(1)}) custom-call(f32[2,64,256]{2,1,0:T(8,128)S(1)} %bitcast.36, f32[16,72,128]{2,1,0:T(8,128)S(1)} %bitcast.33), custom_call_target="tpu_custom_call" | custom-call | tf_op jit(solution)/shard_map/pallas_call | solution.py:61
  109.4 12.2 %all-gather.3.projected = f32[1024,128]{1,0:T(8,128)S(1)} all-gather(f32[256,128]{1,0:T(8,128)S(1)} %get-tuple-element.37), channel_id=5, replica_groups={{0,2,4,6},{8,10,12,14},{1,3,5,7},{9,11,13,15},{16,18,20,22},{24,26,28,3..., dimensions={0}, use_global_device_ids=true | all-gather | bytes 655360 | tf_op jit(solution)/shard_map/all_gather | solution.py:196
  121.7 1.2 shard_map.77
  122.9 6.1 %all-gather.4 = f32[128,128]{1,0:T(8,128)S(1)} all-gather(f32[64,128]{1,0:T(8,128)S(1)} %shard_map.77), channel_id=6, replica_groups=mesh['groups'=2,'rows'=16,'cols'=8,'depth'=2] {'depth'}, dimensions={0}, use_global_device_ids=true | all-gather | bytes 98304 | tf_op jit(solution)/shard_map/all_gather | solution.py:199
  129.0 4.8 %shard_map.78 = (f32[64,128]{1,0:T(8,128)S(1)}, f32[16,64]{1,0:T(8,128)}, f32[16,64]{1,0:T(8,128)}, f32[256,16]{1,0:T(8,128)S(1)}) custom-call(f32[2,64,128]{2,1,0:T(8,128)S(1)} %bitcast.37, f32[1024,128]{1,0:T(8,128)S(1)} %all-gather.3.projected, f32[64,256]{1,0:T(8,128)S(1)} %get-tuple-element.38.one, f32[16,256]{1,0:T(8,128)S(1)} %fusion.one_pick, ...), custom_call_target="tpu_custom_call" | custom-call | tf_op jit(solution)/shard_map/pallas_call | solution.py:61
  133.8 0.1 reshape.52
  133.9 1.9 %all_gather.55 = f32[32,256]{1,0:T(8,128)S(1)} all-gather(f32[16,256]{1,0:T(8,128)S(1)} %reshape.52), channel_id=1, replica_groups=mesh['groups'=2,'rows'=16,'cols'=8,'depth'=2] {'depth'}, dimensions={0}, use_global_device_ids=true | all-gather | bytes 49152 | tf_op jit(solution)/shard_map/all_gather | solution.py:216
  135.8 0.2 fusion.5
  136.0 10.8 %all_to_all.16 = f32[8,32,128]{2,1,0:T(8,128)S(1)} all-to-all(f32[8,32,128]{2,1,0:T(8,128)S(1)} %broadcast_in_dim.13), channel_id=1, replica_groups=mesh['groups'=2,'rows'=16,'cols'=8,'depth'=2] {'cols'}, dimensions={0} | all-to-all | bytes 262144 | tf_op jit(solution)/shard_map/all_to_all | solution.py:24
  146.9 0.7 broadcast_in_dim.14
  147.6 4.0 %all-to-all-start.2 = ((f32[16,32,128]{2,1,0:T(8,128)}), f32[16,32,128]{2,1,0:T(8,128)S(1)}, u32[]{:S(2)}, u32[]{:S(2)}) async-start(f32[16,32,128]{2,1,0:T(8,128)} %broadcast_in_dim.14), calls=%async_computation.2 | async-start | bytes 524288 | tf_op jit(solution)/shard_map/all_to_all | solution.py:24
  151.6 0.7 fusion.7
  152.2 3.5 %all-gather.6 = f32[128,1024]{1,0:T(8,128)S(1)} all-gather(f32[64,1024]{1,0:T(8,128)S(1)} %fusion.7), channel_id=8, replica_groups=mesh['groups'=2,'rows'=16,'cols'=8,'depth'=2] {'depth'}, dimensions={0}, use_global_device_ids=true | all-gather | bytes 786432 | tf_op jit(solution)/shard_map/all_gather | solution.py:231
  155.7 0.3 reshape.53
  156.0 1.9 %copy.32 = f32[64,64,2,16]{1,3,2,0:T(8,128)} copy(f32[64,64,2,16]{0,3,1,2:T(8,128)S(1)} %bitcast.39) | data formatting | bytes 1048576 | tf_op jit(solution)/shard_map/transpose | solution.py:233
  157.9 6.1 %all-to-all-done.2 = f32[16,32,128]{2,1,0:T(8,128)S(1)} async-done(((f32[16,32,128]{2,1,0:T(8,128)}), f32[16,32,128]{2,1,0:T(8,128)S(1)}, u32[]{:S(2)}, u32[]{:S(2)}) %all-to-all-start.2) | async-done | bytes 262176 | tf_op jit(solution)/shard_map/all_to_all | solution.py:24
  164.0 0.1 fusion.6
  164.1 8.4 %all-gather.5 = f32[64,32]{1,0:T(8,128)S(1)} all-gather(f32[32,32]{1,0:T(8,128)S(1)} %fusion.6), channel_id=7, replica_groups=mesh['groups'=2,'rows'=16,'cols'=8,'depth'=2] {'depth'}, dimensions={0}, use_global_device_ids=true | all-gather | bytes 12288 | tf_op jit(solution)/shard_map/all_gather | solution.py:223
  172.5 1.1 shard_map.79
  173.6 0.7 copy.33
  (17 shorter events, 0.1 us)
Async XLA Ops:
  0.6 1.5 copy-start
  0.7 0.7 copy-start.2
  1.4 0.7 copy-start.3
  2.1 0.7 copy-start.1
  147.6 16.4 %all-to-all-start.2 = ((f32[16,32,128]{2,1,0:T(8,128)}), f32[16,32,128]{2,1,0:T(8,128)S(1)}, u32[]{:S(2)}, u32[]{:S(2)}) async-start(f32[16,32,128]{2,1,0:T(8,128)} %broadcast_in_dim.14), calls=%async_computation.2 | async-start | bytes 524288 | tf_op jit(solution)/shard_map/all_to_all | solution.py:24

commit v5 on v4

--- a/solution.py
+++ b/solution.py
@@ -67,19 +67,27 @@
     )(*operands)
 
 
+def class_matrices(got, size_one, slices):
+    return [
+        got[:, c * size_one : (c + 1) * size_one, :].reshape(-1, got.shape[2])
+        for c in range(slices)
+    ]
+
+
 def first_mode(size_one, slices, got, two_old, z_part):
     packed = got[:, slices * size_one :, :]
     width = packed.shape[2] // 2
     one_old = jnp.stack([packed[:, :, :width], packed[:, :, width:]], axis=1)
     one_old = one_old.reshape(-1, width)
     two = two_old[...]
-    total = None
-    for c in range(slices):
-        matrix = got[:, c * size_one : (c + 1) * size_one, :].reshape(-1, two.shape[0])
-        unfolded = mul(matrix, two)
-        term = mul_nt(mul_tn(one_old, unfolded), unfolded)
-        total = term if total is None else total + term
-    z_part[...] = total
+    none = jnp.zeros_like(two)
+    twice = jnp.concatenate(
+        [jnp.concatenate([two, none], axis=1), jnp.concatenate([none, two], axis=1)], axis=0
+    )
+    whole = class_matrices(got, size_one, slices)
+    pairs = [jnp.concatenate(whole[c : c + 2], axis=1) for c in range(0, slices, 2)]
+    unfolded = jnp.concatenate([mul(pair, twice) for pair in pairs], axis=1)
+    z_part[...] = mul_nt(mul(one_old.T, unfolded), unfolded)
 
 
 def to_second(size_one, slices, z_parts, got, one, projected):
@@ -87,33 +95,40 @@
     new = mul(orth_factor(mul_nt(z, z)), z)
     one[...] = new
     rank = new.shape[0]
+    width = got.shape[2]
+    wide = mul(new, jnp.concatenate(class_matrices(got, size_one, slices), axis=1))
     for c in range(slices):
-        matrix = got[:, c * size_one : (c + 1) * size_one, :].reshape(new.shape[1], -1)
-        projected[c * rank : (c + 1) * rank, :] = mul(new, matrix)
+        projected[c * rank : (c + 1) * rank, :] = wide[:, c * width : (c + 1) * width]
 
 
 def second_mode(projected, two_old, z_part):
-    z_part[...] = mul_tn(mul(projected[...], two_old[...]), projected[...])
-
-
-def to_third(z_parts, projected, one, one_pick, two_pick, two, one_own, two_own, spread):
+    z_part[...] = mul(mul_nt(two_old[...].T, projected[...]), projected[...])
+
+
+def to_third(z_parts, projected, one, two, one_own, two_own, spread):
     z = jnp.sum(z_parts[...], axis=0)
     new = mul(orth_factor(mul_nt(z, z)), z)
     two[...] = new
-    first = mul_nt(one_pick[...], one[...])
-    second = mul_nt(two_pick[...], new)
-    one_own[...] = first * math.sqrt(one.shape[1])
-    two_own[...] = second * math.sqrt(new.shape[1])
-    joined = mul(second, new)
-    rank = first.shape[1]
-    for c in range(projected.shape[0] // rank):
-        grid = mul(first, projected[c * rank : (c + 1) * rank, :])
-        spread[c * first.shape[0] : (c + 1) * first.shape[0], :] = mul_nt(grid, joined)
+    rank, length_one = one.shape
+    length_two = new.shape[1]
+    size_one, size_two = one_own.shape[0], two_own.shape[0]
+    first = mul_nt(own_rows("rows", size_one, length_one), one[...])
+    second = mul_nt(own_rows("cols", size_two, length_two), new)
+    one_own[...] = first * math.sqrt(length_one)
+    two_own[...] = second * math.sqrt(length_two)
+    held = projected.shape[0] // rank
+    wide = jnp.concatenate(
+        [projected[c * rank : (c + 1) * rank, :] for c in range(held)], axis=1
+    )
+    wide = mul(first, wide)
+    tall = jnp.concatenate(
+        [wide[:, c * length_two : (c + 1) * length_two] for c in range(held)], axis=0
+    )
+    spread[...] = mul_nt(tall, mul(second, new))
 
 
 def last_orth(scale, grams, z, three):
-    factor = orth_factor(jnp.sum(grams[...], axis=0))
-    three[...] = mul_tn(z[...], factor) * scale
+    three[...] = mul(orth_factor(jnp.sum(grams[...], axis=0)), z[...]) * scale
 
 
 def own_rows(axis, size, length):
@@ -141,8 +156,6 @@
     rank_three = start_three.shape[1]
     rows, cols, depth = (lax.axis_size(name) for name in ("rows", "cols", "depth"))
     length_one, length_two, length_three = size_one * rows, size_two * cols, size_three * depth
-    one_pick = own_rows("rows", size_one, length_one)
-    two_pick = own_rows("cols", size_two, length_two)
     teams = [list(range(first, first + CLASSES)) for first in range(0, cols, CLASSES)]
     half_team = CLASSES // 2
     near = [
@@ -169,9 +182,9 @@
         [thinned, jnp.broadcast_to(two_packed[None], (cols * depth, *two_packed.shape))], axis=1
     )
     one_packed = halves_side_by_side(start_one)
-    got, one_packed, flat, one_pick, two_pick = alone(
+    got, one_packed, flat = alone(
         lambda shard: lax.all_to_all(shard, ("cols", "depth"), 0, 0, tiled=True),
-        message, one_packed, flat, one_pick, two_pick,
+        message, one_packed, flat,
     )
     got = got.reshape(cols, depth, *got.shape[1:])
     own = got[:, :, :lines].sum(axis=1).reshape(cols, slices * size_one, size_two)
@@ -210,8 +223,6 @@
         z_parts,
         projected,
         one,
-        one_pick,
-        two_pick,
     )
     spread = lax.all_gather(spread.reshape(half, -1), "depth", axis=0, tiled=True)
     z_part = mul(spread, flat)
@@ -223,7 +234,7 @@
     grams = lax.all_gather(mul(z_three, z_three.T), "depth")
     three = kernel_call(
         functools.partial(last_orth, math.sqrt(length_three)),
-        (size_three, rank_three),
+        (rank_three, size_three),
         grams,
         z_three,
     )
@@ -231,7 +242,7 @@
     core = lax.all_gather(mul(two, projected.T), "depth")
     core = core.reshape(depth, rank_two, -1, rank_one)
     core = core.transpose(3, 1, 0, 2).reshape(rank_one, rank_two, rank_three)
-    return one_own, two_own, three, core
+    return one_own, two_own, three.T, core
 
 
 def solution(mesh):

time: 175 us -> 170 us (0.971)
  Pallas kernels: 11.1 us -> 8.12 us
  local copies, waits for them, and re-layouts: 6.16 us -> 4.4 us
    pallas_call x5, Pallas kernels: 11.1 us -> 8.12 us  [kernel_call(): pl.pallas_call(kernel, out_shape=outs[0] if one else outs, in_specs=[whol...]
    unnamed x9 -> x6, local copies, waits for them, and re-layouts: 2.65 us -> 0.14 us
where the time goes in v5:
time: 170 us; the launch traced here: 169 us
  blocking collectives  145 us (85%)
  Pallas kernels  8.12 us (5%)
  waiting for transfers between devices  5.93 us (3%)
  local copies, waits for them, and re-layouts  4.4 us (3%)
  starting transfers between devices  3.97 us (2%)
    all_to_all x1, blocking collectives, body(): lax.all_to_all(shard, ('cols', 'depth'), 0, 0, tiled=True)  53.1 us
    all_gather x1, blocking collectives, body(): got = lax.all_gather(jnp.concatenate([own, one_packed], axis=0), 'rows')  28.6 us
    all_gather x1, blocking collectives, body(): lax.all_gather(z_part, ('cols', 'depth'), axis_index_groups=near)  12.8 us
    all_gather x1, blocking collectives, body(): projected = lax.all_gather(projected, 'cols', axis_index_groups=teams)  12.2 us
    all_to_all x1, blocking collectives, from_everyone(): lax.all_to_all(jnp.broadcast_to(shard[None], (peers, *shard.shape)), axis...  10.7 us
    all_gather x1, blocking collectives, body(): grams = lax.all_gather(mul(z_three, z_three.T), 'depth')  8.47 us
    pallas_call x5, Pallas kernels, kernel_call(): pl.pallas_call(kernel, out_shape=outs[0] if one else outs, in_specs=[whol...  8.12 us
    all_gather x1, blocking collectives, body(): z_parts = lax.all_gather(z_part, 'cols', axis_index_groups=far)  7.03 us
  transfers between devices with their start and end apart: 1, of which 1 were waited for; matrix products, arithmetic and copies ran while one was open for 2% of the time, Pallas kernels for 0%

profile of v5, /device:TPU:65, one launch (start us, length us, event | category | flops | bytes accessed | tf_op | source)
XLA Modules:
  0.0 169.4 jit_solution(14163777913765812289)
XLA Ops:
  0.6 0.0 copy-start
  0.6 0.0 copy-start.2
  0.7 0.0 copy-start.1
  0.7 0.8 fusion
  1.4 0.0 copy-done.2
  1.4 0.1 copy-done
  1.6 0.0 copy-done.1
  1.6 0.2 fusion.2
  1.8 0.1 pad_maximum_fusion.4
  1.9 0.1 pad_maximum_fusion.3
  2.0 53.1 %all_to_all.15 = f32[16,16,128]{2,1,0:T(8,128)S(1)} all-to-all(f32[16,16,128]{2,1,0:T(8,128)S(1)} %pad_maximum_fusion), channel_id=1, replica_groups=mesh['groups'=2,'rows'=16,'cols'=8,'depth'=2] {'cols','depth'}, dimensions={0} | all-to-all | bytes 262144 | tf_op jit(solution)/shard_map/all_to_all | solution.py:186
  55.1 0.1 slice_bitcast_fusion.1
  55.2 0.1 copy.26
  55.3 0.1 reshape.48
  55.5 0.1 copy.25
  55.6 0.1 pad_maximum_fusion.1
  55.7 0.1 copy.27
  55.8 28.6 %all-gather = f32[1152,128]{1,0:T(8,128)S(1)} all-gather(f32[72,128]{1,0:T(8,128)S(1)} %copy.27), channel_id=2, replica_groups=mesh['groups'=2,'rows'=16,'cols'=8,'depth'=2] {'rows'}, dimensions={0}, use_global_device_ids=true | all-gather | bytes 626688 | tf_op jit(solution)/shard_map/all_gather | solution.py:194
  84.4 1.5 shard_map.75
  85.9 12.8 %all-gather.1 = f32[256,256]{1,0:T(8,128)S(1)} all-gather(f32[64,256]{1,0:T(8,128)S(1)} %shard_map.75), channel_id=3, replica_groups={{0,1,2,3},{4,5,6,7},{8,9,10,11},{12,13,14,15},{16,17,18,19},{20,21,22,2..., dimensions={0}, use_global_device_ids=true | all-gather | bytes 327680 | tf_op jit(solution)/shard_map/all_gather | solution.py:200
  98.7 7.0 %all-gather.2 = f32[128,256]{1,0:T(8,128)S(1)} all-gather(f32[64,256]{1,0:T(8,128)S(1)} %reduce_sum.37), channel_id=4, replica_groups={{0,4},{2,6},{8,12},{10,14},{1,5},{3,7},{9,13},{11,15},{16,20},{18,22},{..., dimensions={0}, use_global_device_ids=true | all-gather | bytes 196608 | tf_op jit(solution)/shard_map/all_gather | solution.py:201
  105.7 1.8 %shard_map.76 = (f32[64,256]{1,0:T(8,128)S(1)}, f32[256,128]{1,0:T(8,128)S(1)}) custom-call(f32[2,64,256]{2,1,0:T(8,128)S(1)} %bitcast.37, f32[16,72,128]{2,1,0:T(8,128)S(1)} %bitcast.34), custom_call_target="tpu_custom_call" | custom-call | tf_op jit(solution)/shard_map/pallas_call | solution.py:61
  107.5 12.2 %all-gather.3.projected = f32[1024,128]{1,0:T(8,128)S(1)} all-gather(f32[256,128]{1,0:T(8,128)S(1)} %get-tuple-element.31), channel_id=5, replica_groups={{0,2,4,6},{8,10,12,14},{1,3,5,7},{9,11,13,15},{16,18,20,22},{24,26,28,3..., dimensions={0}, use_global_device_ids=true | all-gather | bytes 655360 | tf_op jit(solution)/shard_map/all_gather | solution.py:209
  119.7 0.9 shard_map.77
  120.7 6.1 %all-gather.4 = f32[128,128]{1,0:T(8,128)S(1)} all-gather(f32[64,128]{1,0:T(8,128)S(1)} %shard_map.77), channel_id=6, replica_groups=mesh['groups'=2,'rows'=16,'cols'=8,'depth'=2] {'depth'}, dimensions={0}, use_global_device_ids=true | all-gather | bytes 98304 | tf_op jit(solution)/shard_map/all_gather | solution.py:212
  126.8 2.2 %shard_map.78 = (f32[64,128]{1,0:T(8,128)S(1)}, f32[16,64]{1,0:T(8,128)}, f32[16,64]{1,0:T(8,128)}, f32[256,16]{1,0:T(8,128)S(1)}) custom-call(f32[2,64,128]{2,1,0:T(8,128)S(1)} %bitcast.38, f32[1024,128]{1,0:T(8,128)S(1)} %all-gather.3.projected, f32[64,256]{1,0:T(8,128)S(1)} %get-tuple-element.32.one), custom_call_target="tpu_custom_call" | custom-call | tf_op jit(solution)/shard_map/pallas_call | solution.py:61
  129.1 0.1 reshape.52
  129.2 1.9 %all_gather.55 = f32[32,256]{1,0:T(8,128)S(1)} all-gather(f32[16,256]{1,0:T(8,128)S(1)} %reshape.52), channel_id=1, replica_groups=mesh['groups'=2,'rows'=16,'cols'=8,'depth'=2] {'depth'}, dimensions={0}, use_global_device_ids=true | all-gather | bytes 49152 | tf_op jit(solution)/shard_map/all_gather | solution.py:227
  131.1 0.2 fusion.3
  131.3 10.7 %all_to_all.16 = f32[8,32,128]{2,1,0:T(8,128)S(1)} all-to-all(f32[8,32,128]{2,1,0:T(8,128)S(1)} %broadcast_in_dim.13), channel_id=1, replica_groups=mesh['groups'=2,'rows'=16,'cols'=8,'depth'=2] {'cols'}, dimensions={0} | all-to-all | bytes 262144 | tf_op jit(solution)/shard_map/all_to_all | solution.py:24
  142.0 0.7 broadcast_in_dim.14
  142.7 4.0 %all-to-all-start.2 = ((f32[16,32,128]{2,1,0:T(8,128)}), f32[16,32,128]{2,1,0:T(8,128)S(1)}, u32[]{:S(2)}, u32[]{:S(2)}) async-start(f32[16,32,128]{2,1,0:T(8,128)} %broadcast_in_dim.14), calls=%async_computation.2 | async-start | bytes 524288 | tf_op jit(solution)/shard_map/all_to_all | solution.py:24
  146.7 0.7 fusion.5
  147.3 3.6 %all-gather.6 = f32[128,1024]{1,0:T(8,128)S(1)} all-gather(f32[64,1024]{1,0:T(8,128)S(1)} %fusion.5), channel_id=8, replica_groups=mesh['groups'=2,'rows'=16,'cols'=8,'depth'=2] {'depth'}, dimensions={0}, use_global_device_ids=true | all-gather | bytes 786432 | tf_op jit(solution)/shard_map/all_gather | solution.py:242
  151.0 0.3 reshape.53
  151.2 1.9 %copy.29 = f32[64,64,2,16]{1,3,2,0:T(8,128)} copy(f32[64,64,2,16]{0,3,1,2:T(8,128)S(1)} %bitcast.40) | data formatting | bytes 1048576 | tf_op jit(solution)/shard_map/transpose | solution.py:244
  153.1 5.9 %all-to-all-done.2 = f32[16,32,128]{2,1,0:T(8,128)S(1)} async-done(((f32[16,32,128]{2,1,0:T(8,128)}), f32[16,32,128]{2,1,0:T(8,128)S(1)}, u32[]{:S(2)}, u32[]{:S(2)}) %all-to-all-start.2) | async-done | bytes 262176 | tf_op jit(solution)/shard_map/all_to_all | solution.py:24
  159.1 0.1 fusion.4
  159.2 8.5 %all-gather.5 = f32[64,32]{1,0:T(8,128)S(1)} all-gather(f32[32,32]{1,0:T(8,128)S(1)} %fusion.4), channel_id=7, replica_groups=mesh['groups'=2,'rows'=16,'cols'=8,'depth'=2] {'depth'}, dimensions={0}, use_global_device_ids=true | all-gather | bytes 12288 | tf_op jit(solution)/shard_map/all_gather | solution.py:234
  167.7 1.7 shard_map.79
  (14 shorter events, 0.1 us)
Async XLA Ops:
  0.6 0.9 copy-start
  0.6 0.8 copy-start.2
  0.7 0.9 copy-start.1
  142.7 16.4 %all-to-all-start.2 = ((f32[16,32,128]{2,1,0:T(8,128)}), f32[16,32,128]{2,1,0:T(8,128)S(1)}, u32[]{:S(2)}, u32[]{:S(2)}) async-start(f32[16,32,128]{2,1,0:T(8,128)} %broadcast_in_dim.14), calls=%async_computation.2 | async-start | bytes 524288 | tf_op jit(solution)/shard_map/all_to_all | solution.py:24

commit v6 on v5

--- a/solution.py
+++ b/solution.py
@@ -114,8 +114,8 @@
     size_one, size_two = one_own.shape[0], two_own.shape[0]
     first = mul_nt(own_rows("rows", size_one, length_one), one[...])
     second = mul_nt(own_rows("cols", size_two, length_two), new)
-    one_own[...] = first * math.sqrt(length_one)
-    two_own[...] = second * math.sqrt(length_two)
+    one_own[...] = first
+    two_own[...] = second
     held = projected.shape[0] // rank
     wide = jnp.concatenate(
         [projected[c * rank : (c + 1) * rank, :] for c in range(held)], axis=1
@@ -127,8 +127,17 @@
     spread[...] = mul_nt(tall, mul(second, new))
 
 
-def last_orth(scale, grams, z, three):
-    three[...] = mul(orth_factor(jnp.sum(grams[...], axis=0)), z[...]) * scale
+def last_orth(scale, parts, three):
+    shares = parts.shape[0]
+    whole = [
+        jnp.concatenate([parts[share, level] for share in range(shares)], axis=0)
+        for level in range(parts.shape[1])
+    ]
+    gram = functools.reduce(jnp.add, [mul_nt(z, z) for z in whole])
+    own = whole[0]
+    for level in range(1, len(whole)):
+        own = jnp.where(lax.axis_index("depth") == level, whole[level], own)
+    three[...] = mul(orth_factor(gram), own) * scale
 
 
 def own_rows(axis, size, length):
@@ -225,24 +234,31 @@
         one,
     )
     spread = lax.all_gather(spread.reshape(half, -1), "depth", axis=0, tiled=True)
-    z_part = mul(spread, flat)
+    shares = jnp.broadcast_to(
+        mul(spread, flat).reshape(1, half_team, -1, size_three),
+        (cols // half_team, half_team, rank_three // half_team, size_three),
+    ).reshape(cols, -1, size_three)
     z_part, two, projected, one_own, two_own = alone(
-        lambda shard: from_everyone(shard, "cols"), z_part, two, projected, one_own, two_own
-    )
-    z_part = z_part.sum(axis=0)
-    z_three = from_everyone(z_part, "rows").sum(axis=0)
-    grams = lax.all_gather(mul(z_three, z_three.T), "depth")
+        lambda shard: lax.all_to_all(shard, "cols", 0, 0, tiled=True),
+        shares, two, projected, one_own, two_own,
+    )
+    z_part = from_everyone(z_part.sum(axis=0), "rows").sum(axis=0)
+    z_parts = lax.all_gather(z_part, ("cols", "depth"), axis_index_groups=near)
     three = kernel_call(
         functools.partial(last_orth, math.sqrt(length_three)),
         (rank_three, size_three),
-        grams,
-        z_three,
+        z_parts.reshape(half_team, depth, -1, size_three),
     )
 
     core = lax.all_gather(mul(two, projected.T), "depth")
     core = core.reshape(depth, rank_two, -1, rank_one)
     core = core.transpose(3, 1, 0, 2).reshape(rank_one, rank_two, rank_three)
-    return one_own, two_own, three.T, core
+    return (
+        one_own * math.sqrt(length_one),
+        two_own * math.sqrt(length_two),
+        three.T,
+        core,
+    )
 
 
 def solution(mesh):

time: 170 us -> 168 us (0.988)
  blocking collectives: 145 us -> 143 us
where the time goes in v6:
time: 168 us; the launch traced here: 167 us
  blocking collectives  143 us (85%)
  Pallas kernels  8.16 us (5%)
  waiting for transfers between devices  4.67 us (3%)
  local copies, waits for them, and re-layouts  4.32 us (3%)
  starting transfers between devices  3.95 us (2%)
    all_to_all x1, blocking collectives, body(): lax.all_to_all(shard, ('cols', 'depth'), 0, 0, tiled=True)  53.1 us
    all_gather x1, blocking collectives, body(): got = lax.all_gather(jnp.concatenate([own, one_packed], axis=0), 'rows')  28.6 us
    all_gather x1, blocking collectives, body(): lax.all_gather(z_part, ('cols', 'depth'), axis_index_groups=near)  12.8 us
    all_gather x1, blocking collectives, body(): projected = lax.all_gather(projected, 'cols', axis_index_groups=teams)  12.2 us
    all_to_all x1, blocking collectives, body(): lax.all_to_all(shard, 'cols', 0, 0, tiled=True)  9.54 us
    all_gather x1, blocking collectives, body(): z_parts = lax.all_gather(z_part, ('cols', 'depth'), axis_index_groups=near)  8.55 us
    pallas_call x5, Pallas kernels, kernel_call(): pl.pallas_call(kernel, out_shape=outs[0] if one else outs, in_specs=[whol...  8.16 us
    all_gather x1, blocking collectives, body(): z_parts = lax.all_gather(z_part, 'cols', axis_index_groups=far)  7.03 us
  transfers between devices with their start and end apart: 1, of which 1 were waited for; matrix products, arithmetic and copies ran while one was open for 2% of the time, Pallas kernels for 0%

profile of v6, /device:TPU:65, one launch (start us, length us, event | category | flops | bytes accessed | tf_op | source)
XLA Modules:
  0.0 167.3 jit_solution(10498695691656592422)
XLA Ops:
  0.6 0.0 copy-start
  0.6 0.0 copy-start.2
  0.7 0.0 copy-start.1
  0.7 0.8 fusion
  1.4 0.0 copy-done.2
  1.4 0.1 copy-done
  1.6 0.0 copy-done.1
  1.6 0.2 fusion.2
  1.8 0.1 pad_maximum_fusion.4
  1.9 0.1 pad_maximum_fusion.3
  2.0 53.1 %all_to_all.15 = f32[16,16,128]{2,1,0:T(8,128)S(1)} all-to-all(f32[16,16,128]{2,1,0:T(8,128)S(1)} %pad_maximum_fusion), channel_id=1, replica_groups=mesh['groups'=2,'rows'=16,'cols'=8,'depth'=2] {'cols','depth'}, dimensions={0} | all-to-all | bytes 262144 | tf_op jit(solution)/shard_map/all_to_all | solution.py:195
  55.1 0.1 slice_bitcast_fusion.1
  55.2 0.1 copy.26
  55.3 0.1 reshape.55
  55.5 0.1 copy.25
  55.6 0.1 pad_maximum_fusion.1
  55.7 0.1 copy.27
  55.8 28.6 %all-gather = f32[1152,128]{1,0:T(8,128)S(1)} all-gather(f32[72,128]{1,0:T(8,128)S(1)} %copy.27), channel_id=2, replica_groups=mesh['groups'=2,'rows'=16,'cols'=8,'depth'=2] {'rows'}, dimensions={0}, use_global_device_ids=true | all-gather | bytes 626688 | tf_op jit(solution)/shard_map/all_gather | solution.py:203
  84.4 1.5 shard_map.75
  85.9 12.8 %all-gather.1 = f32[256,256]{1,0:T(8,128)S(1)} all-gather(f32[64,256]{1,0:T(8,128)S(1)} %shard_map.75), channel_id=3, replica_groups={{0,1,2,3},{4,5,6,7},{8,9,10,11},{12,13,14,15},{16,17,18,19},{20,21,22,2..., dimensions={0}, use_global_device_ids=true | all-gather | bytes 327680 | tf_op jit(solution)/shard_map/all_gather | solution.py:209
  98.7 7.0 %all-gather.2 = f32[128,256]{1,0:T(8,128)S(1)} all-gather(f32[64,256]{1,0:T(8,128)S(1)} %reduce_sum.37), channel_id=4, replica_groups={{0,4},{2,6},{8,12},{10,14},{1,5},{3,7},{9,13},{11,15},{16,20},{18,22},{..., dimensions={0}, use_global_device_ids=true | all-gather | bytes 196608 | tf_op jit(solution)/shard_map/all_gather | solution.py:210
  105.7 1.8 %shard_map.76 = (f32[64,256]{1,0:T(8,128)S(1)}, f32[256,128]{1,0:T(8,128)S(1)}) custom-call(f32[2,64,256]{2,1,0:T(8,128)S(1)} %bitcast.37, f32[16,72,128]{2,1,0:T(8,128)S(1)} %bitcast.34), custom_call_target="tpu_custom_call" | custom-call | tf_op jit(solution)/shard_map/pallas_call | solution.py:61
  107.5 12.2 %all-gather.3.projected = f32[1024,128]{1,0:T(8,128)S(1)} all-gather(f32[256,128]{1,0:T(8,128)S(1)} %get-tuple-element.31), channel_id=5, replica_groups={{0,2,4,6},{8,10,12,14},{1,3,5,7},{9,11,13,15},{16,18,20,22},{24,26,28,3..., dimensions={0}, use_global_device_ids=true | all-gather | bytes 655360 | tf_op jit(solution)/shard_map/all_gather | solution.py:218
  119.7 0.9 shard_map.77
  120.7 6.1 %all-gather.4 = f32[128,128]{1,0:T(8,128)S(1)} all-gather(f32[64,128]{1,0:T(8,128)S(1)} %shard_map.77), channel_id=6, replica_groups=mesh['groups'=2,'rows'=16,'cols'=8,'depth'=2] {'depth'}, dimensions={0}, use_global_device_ids=true | all-gather | bytes 98304 | tf_op jit(solution)/shard_map/all_gather | solution.py:221
  126.8 2.0 %shard_map.78 = (f32[64,128]{1,0:T(8,128)S(1)}, f32[16,64]{1,0:T(8,128)S(1)}, f32[16,64]{1,0:T(8,128)S(1)}, f32[256,16]{1,0:T(8,128)S(1)}) custom-call(f32[2,64,128]{2,1,0:T(8,128)S(1)} %bitcast.38, f32[1024,128]{1,0:T(8,128)S(1)} %all-gather.3.projected, f32[64,256]{1,0:T(8,128)S(1)} %get-tuple-element.32.one), custom_call_target="tpu_custom_call" | custom-call | tf_op jit(solution)/shard_map/pallas_call | solution.py:61
  128.8 0.1 reshape.59
  128.9 1.9 %all_gather.55 = f32[32,256]{1,0:T(8,128)S(1)} all-gather(f32[16,256]{1,0:T(8,128)S(1)} %reshape.59), channel_id=1, replica_groups=mesh['groups'=2,'rows'=16,'cols'=8,'depth'=2] {'depth'}, dimensions={0}, use_global_device_ids=true | all-gather | bytes 49152 | tf_op jit(solution)/shard_map/all_gather | solution.py:236
  130.8 0.2 fusion.3
  131.0 9.5 %all_to_all.16 = f32[8,16,128]{2,1,0:T(8,128)S(1)} all-to-all(f32[8,16,128]{2,1,0:T(8,128)S(1)} %bitcast.47), channel_id=1, replica_groups=mesh['groups'=2,'rows'=16,'cols'=8,'depth'=2] {'cols'}, dimensions={0} | all-to-all | bytes 131072 | tf_op jit(solution)/shard_map/all_to_all | solution.py:242
  140.6 0.6 broadcast_in_dim.31
  141.2 4.0 %all-to-all-start.2 = ((f32[16,16,128]{2,1,0:T(8,128)}), f32[16,16,128]{2,1,0:T(8,128)S(1)}, u32[]{:S(2)}, u32[]{:S(2)}) async-start(f32[16,16,128]{2,1,0:T(8,128)} %broadcast_in_dim.31), calls=%async_computation.2 | async-start | bytes 262144 | tf_op jit(solution)/shard_map/all_to_all | solution.py:24
  145.2 0.7 fusion.4
  145.9 3.5 %all-gather.6 = f32[128,1024]{1,0:T(8,128)S(1)} all-gather(f32[64,1024]{1,0:T(8,128)S(1)} %fusion.4), channel_id=8, replica_groups=mesh['groups'=2,'rows'=16,'cols'=8,'depth'=2] {'depth'}, dimensions={0}, use_global_device_ids=true | all-gather | bytes 786432 | tf_op jit(solution)/shard_map/all_gather | solution.py:253
  149.4 0.3 reshape.62
  149.7 1.9 %copy.29 = f32[64,64,2,16]{1,3,2,0:T(8,128)} copy(f32[64,64,2,16]{0,3,1,2:T(8,128)S(1)} %bitcast.40) | data formatting | bytes 1048576 | tf_op jit(solution)/shard_map/transpose | solution.py:255
  151.6 0.6 broadcast_multiply_fusion
  152.2 4.7 %all-to-all-done.2 = f32[16,16,128]{2,1,0:T(8,128)S(1)} async-done(((f32[16,16,128]{2,1,0:T(8,128)}), f32[16,16,128]{2,1,0:T(8,128)S(1)}, u32[]{:S(2)}, u32[]{:S(2)}) %all-to-all-start.2) | async-done | bytes 131104 | tf_op jit(solution)/shard_map/all_to_all | solution.py:24
  156.9 8.5 %all-gather.5 = f32[64,128]{1,0:T(8,128)S(1)} all-gather(f32[16,128]{1,0:T(8,128)S(1)} %reduce_sum.39), channel_id=7, replica_groups={{0,1,2,3},{4,5,6,7},{8,9,10,11},{12,13,14,15},{16,17,18,19},{20,21,22,2..., dimensions={0}, use_global_device_ids=true | all-gather | bytes 40960 | tf_op jit(solution)/shard_map/all_gather | solution.py:246
  165.4 2.0 %shard_map.79 = f32[32,128]{1,0:T(8,128)} custom-call(f32[2,2,16,128]{3,2,1,0:T(8,128)S(1)} %bitcast.39), custom_call_target="tpu_custom_call" | custom-call | tf_op jit(solution)/shard_map/pallas_call | solution.py:61
  (14 shorter events, 0.1 us)
Async XLA Ops:
  0.6 0.9 copy-start
  0.6 0.8 copy-start.2
  0.7 0.9 copy-start.1
  141.2 15.6 %all-to-all-start.2 = ((f32[16,16,128]{2,1,0:T(8,128)}), f32[16,16,128]{2,1,0:T(8,128)S(1)}, u32[]{:S(2)}, u32[]{:S(2)}) async-start(f32[16,16,128]{2,1,0:T(8,128)} %broadcast_in_dim.31), calls=%async_computation.2 | async-start | bytes 262144 | tf_op jit(solution)/shard_map/all_to_all | solution.py:24

commit v7 on v6

--- a/solution.py
+++ b/solution.py
@@ -11,6 +11,7 @@
 NEWTON = 3
 LANES = 128
 CLASSES = 4
+EVERYWHERE = ("rows", "cols", "depth")
 KERNEL_BYTES = 8 * 2**20
 exact_mode = lax.Precision.HIGHEST
 
@@ -165,8 +166,24 @@
     rank_three = start_three.shape[1]
     rows, cols, depth = (lax.axis_size(name) for name in ("rows", "cols", "depth"))
     length_one, length_two, length_three = size_one * rows, size_two * cols, size_three * depth
-    teams = [list(range(first, first + CLASSES)) for first in range(0, cols, CLASSES)]
     half_team = CLASSES // 2
+
+    def core_of(half, row, col):
+        return (half + row + col) % depth
+
+    blocks = [
+        [(row * cols + col) * depth + core_of(half, row, col) for col in range(cols) for half in range(depth)]
+        for row in range(rows)
+    ]
+    chips = [order[at : at + depth] for order in blocks for at in range(0, cols * depth, depth)]
+    lines_of_chips = [
+        [row * depth + core_of(half, row, 0) for row in range(rows)] for half in range(depth)
+    ]
+    teams = [
+        [col * depth + core_of(half, 0, col) for col in range(first, first + CLASSES)]
+        for first in range(0, cols, CLASSES)
+        for half in range(depth)
+    ]
     near = [
         list(range(first * depth, (first + half_team) * depth))
         for first in range(0, cols, half_team)
@@ -185,14 +202,16 @@
     lines = thinned.shape[3]
     two_packed = halves_side_by_side(start_two)
     thinned = jnp.broadcast_to(
-        thinned.transpose(0, 2, 1, 3, 4), (len(teams), CLASSES, depth, lines, LANES)
+        thinned.transpose(0, 2, 1, 3, 4), (cols // CLASSES, CLASSES, depth, lines, LANES)
     ).reshape(cols * depth, lines, LANES)
     message = jnp.concatenate(
         [thinned, jnp.broadcast_to(two_packed[None], (cols * depth, *two_packed.shape))], axis=1
     )
     one_packed = halves_side_by_side(start_one)
     got, one_packed, flat = alone(
-        lambda shard: lax.all_to_all(shard, ("cols", "depth"), 0, 0, tiled=True),
+        lambda shard: lax.all_to_all(
+            shard, EVERYWHERE, 0, 0, tiled=True, axis_index_groups=blocks
+        ),
         message, one_packed, flat,
     )
     got = got.reshape(cols, depth, *got.shape[1:])
@@ -200,7 +219,11 @@
     own = own.transpose(1, 0, 2).reshape(slices * size_one, length_two)
     two_old = halves_stacked(got[:, 0, lines:])
 
-    got = lax.all_gather(jnp.concatenate([own, one_packed], axis=0), "rows")
+    got = lax.all_gather(
+        jnp.concatenate([own, one_packed], axis=0),
+        ("rows", "depth"),
+        axis_index_groups=lines_of_chips,
+    )
 
     cut = (size_one, slices)
     z_part = kernel_call(
@@ -215,7 +238,7 @@
         z_parts,
         got,
     )
-    projected = lax.all_gather(projected, "cols", axis_index_groups=teams)
+    projected = lax.all_gather(projected, ("cols", "depth"), axis_index_groups=teams)
     projected = projected.reshape(-1, length_two)
     z_part = kernel_call(second_mode, (rank_two, length_two), projected, two_old)
     z_parts = lax.all_gather(z_part, "depth")
@@ -233,7 +256,8 @@
         projected,
         one,
     )
-    spread = lax.all_gather(spread.reshape(half, -1), "depth", axis=0, tiled=True)
+    spread = lax.all_gather(spread.reshape(half, -1), EVERYWHERE, axis_index_groups=chips)
+    spread = spread.reshape(rank_three, -1)
     shares = jnp.broadcast_to(
         mul(spread, flat).reshape(1, half_team, -1, size_three),
         (cols // half_team, half_team, rank_three // half_team, size_three),
@@ -250,7 +274,9 @@
         z_parts.reshape(half_team, depth, -1, size_three),
     )
 
-    core = lax.all_gather(mul(two, projected.T), "depth")
+    core = lax.all_gather(
+        mul(two, projected.T), EVERYWHERE, axis_index_groups=chips
+    )
     core = core.reshape(depth, rank_two, -1, rank_one)
     core = core.transpose(3, 1, 0, 2).reshape(rank_one, rank_two, rank_three)
     return (

time: 168 us -> 164 us (0.976)
  blocking collectives: 143 us -> 139 us
    all_gather x4, blocking collectives: 46.3 us -> 53.1 us  [the longest x1 32.4 us: body(): lax.all_gather(jnp.concatenate([own, one_packed], axis=0), ('rows', 'dept...]
    all_gather x1, blocking collectives: 12.8 us -> 6.07 us  [body(): lax.all_gather(z_part, ('cols', 'depth'), axis_index_groups=near)]
    all_gather x1, blocking collectives: 6.15 us -> 1.95 us  [body(): z_parts = lax.all_gather(z_part, 'depth')]
where the time goes in v7:
time: 164 us; the launch traced here: 163 us
  blocking collectives  139 us (85%)
  Pallas kernels  8.15 us (5%)
  waiting for transfers between devices  4.62 us (3%)
  local copies, waits for them, and re-layouts  4.32 us (3%)
  starting transfers between devices  3.95 us (2%)
    all_to_all x1, blocking collectives, body(): lax.all_to_all(shard, EVERYWHERE, 0, 0, tiled=True, axis_index_groups=blo...  53.1 us
    all_gather x1, blocking collectives, body(): lax.all_gather(jnp.concatenate([own, one_packed], axis=0), ('rows', 'dept...  32.4 us
    all_gather x1, blocking collectives, body(): lax.all_gather(projected, ('cols', 'depth'), axis_index_groups=teams)  15.3 us
    all_to_all x1, blocking collectives, body(): lax.all_to_all(shard, 'cols', 0, 0, tiled=True)  9.55 us
    all_gather x1, blocking collectives, body(): z_parts = lax.all_gather(z_part, ('cols', 'depth'), axis_index_groups=near)  8.59 us
    pallas_call x5, Pallas kernels, kernel_call(): pl.pallas_call(kernel, out_shape=outs[0] if one else outs, in_specs=[whol...  8.15 us
    all_gather x1, blocking collectives, body(): z_parts = lax.all_gather(z_part, 'cols', axis_index_groups=far)  6.88 us
    all_gather x1, blocking collectives, body(): lax.all_gather(z_part, ('cols', 'depth'), axis_index_groups=near)  6.07 us
  transfers between devices with their start and end apart: 1, of which 1 were waited for; matrix products, arithmetic and copies ran while one was open for 2% of the time, Pallas kernels for 0%

profile of v7, /device:TPU:65, one launch (start us, length us, event | category | flops | bytes accessed | tf_op | source)
XLA Modules:
  0.0 163.2 jit_solution(18023415897806967694)
XLA Ops:
  0.6 0.0 copy-start
  0.6 0.0 copy-start.2
  0.7 0.0 copy-start.1
  0.7 0.8 fusion.2
  1.4 0.0 copy-done.2
  1.4 0.1 copy-done
  1.6 0.0 copy-done.1
  1.6 0.2 fusion.4
  1.8 0.1 pad_maximum_fusion.4
  1.9 0.1 pad_maximum_fusion.3
  2.0 53.1 %all_to_all.15 = f32[16,16,128]{2,1,0:T(8,128)S(1)} all-to-all(f32[16,16,128]{2,1,0:T(8,128)S(1)} %pad_maximum_fusion), channel_id=1, replica_groups={{0,1,3,2,4,5,7,6,8,9,11,10,12,13,15,14},{17,16,18,19,21,20,22,23,25,24,..., dimensions={0} | all-to-all | bytes 262144 | tf_op jit(solution)/shard_map/all_to_all | solution.py:212
  55.1 0.1 slice_bitcast_fusion.1
  55.2 0.1 copy.26
  55.3 0.1 reshape.58
  55.5 0.1 copy.25
  55.6 0.1 pad_maximum_fusion.1
  55.7 0.1 copy.27
  55.7 32.4 %all-gather = f32[1152,128]{1,0:T(8,128)S(1)} all-gather(f32[72,128]{1,0:T(8,128)S(1)} %copy.27), channel_id=2, replica_groups={{0,17,32,49,64,81,96,113,128,145,160,177,192,209,224,241},{1,16,33,48,6..., dimensions={0}, use_global_device_ids=true | all-gather | bytes 626688 | tf_op jit(solution)/shard_map/all_gather | solution.py:222
  88.2 1.5 shard_map.75
  89.6 6.1 %all-gather.1 = f32[256,256]{1,0:T(8,128)S(1)} all-gather(f32[64,256]{1,0:T(8,128)S(1)} %shard_map.75), channel_id=3, replica_groups={{0,1,2,3},{4,5,6,7},{8,9,10,11},{12,13,14,15},{16,17,18,19},{20,21,22,2..., dimensions={0}, use_global_device_ids=true | all-gather | bytes 327680 | tf_op jit(solution)/shard_map/all_gather | solution.py:232
  95.7 6.9 %all-gather.2 = f32[128,256]{1,0:T(8,128)S(1)} all-gather(f32[64,256]{1,0:T(8,128)S(1)} %reduce_sum.37), channel_id=4, replica_groups={{0,4},{2,6},{8,12},{10,14},{1,5},{3,7},{9,13},{11,15},{16,20},{18,22},{..., dimensions={0}, use_global_device_ids=true | all-gather | bytes 196608 | tf_op jit(solution)/shard_map/all_gather | solution.py:233
  102.6 1.8 %shard_map.76 = (f32[64,256]{1,0:T(8,128)S(1)}, f32[256,128]{1,0:T(8,128)S(1)}) custom-call(f32[2,64,256]{2,1,0:T(8,128)S(1)} %bitcast.38, f32[16,72,128]{2,1,0:T(8,128)S(1)} %bitcast.35), custom_call_target="tpu_custom_call" | custom-call | tf_op jit(solution)/shard_map/pallas_call | solution.py:62
  104.4 15.3 %all-gather.3.projected = f32[1024,128]{1,0:T(8,128)S(1)} all-gather(f32[256,128]{1,0:T(8,128)S(1)} %get-tuple-element.31), channel_id=5, replica_groups={{0,3,4,7},{1,2,5,6},{8,11,12,15},{9,10,13,14},{16,19,20,23},{17,18,21,2..., dimensions={0}, use_global_device_ids=true | all-gather | bytes 655360 | tf_op jit(solution)/shard_map/all_gather | solution.py:241
  119.7 0.9 shard_map.77
  120.6 1.9 %all-gather.4 = f32[128,128]{1,0:T(8,128)S(1)} all-gather(f32[64,128]{1,0:T(8,128)S(1)} %shard_map.77), channel_id=6, replica_groups=mesh['groups'=2,'rows'=16,'cols'=8,'depth'=2] {'depth'}, dimensions={0}, use_global_device_ids=true | all-gather | bytes 98304 | tf_op jit(solution)/shard_map/all_gather | solution.py:244
  122.6 2.0 %shard_map.78 = (f32[64,128]{1,0:T(8,128)S(1)}, f32[16,64]{1,0:T(8,128)S(1)}, f32[16,64]{1,0:T(8,128)S(1)}, f32[256,16]{1,0:T(8,128)S(1)}) custom-call(f32[2,64,128]{2,1,0:T(8,128)S(1)} %bitcast.39, f32[1024,128]{1,0:T(8,128)S(1)} %all-gather.3.projected, f32[64,256]{1,0:T(8,128)S(1)} %get-tuple-element.32.one), custom_call_target="tpu_custom_call" | custom-call | tf_op jit(solution)/shard_map/pallas_call | solution.py:62
  124.6 0.1 all_gather_reshape.3
  124.7 1.9 %all_gather.55 = f32[2,16,256]{2,1,0:T(8,128)S(1)} all-gather(f32[1,16,256]{2,1,0:T(8,128)S(1)} %all_gather_reshape.3), channel_id=1, replica_groups={{0,1},{3,2},{4,5},{7,6},{8,9},{11,10},{12,13},{15,14},{17,16},{18,19},{..., dimensions={0}, use_global_device_ids=true | all-gather | bytes 49152 | tf_op jit(solution)/shard_map/all_gather | solution.py:259
  126.6 0.2 fusion
  126.8 9.5 %all_to_all.16 = f32[8,16,128]{2,1,0:T(8,128)S(1)} all-to-all(f32[8,16,128]{2,1,0:T(8,128)S(1)} %bitcast.48), channel_id=1, replica_groups=mesh['groups'=2,'rows'=16,'cols'=8,'depth'=2] {'cols'}, dimensions={0} | all-to-all | bytes 131072 | tf_op jit(solution)/shard_map/all_to_all | solution.py:266
  136.4 0.6 broadcast_in_dim.28
  137.0 4.0 %all-to-all-start.2 = ((f32[16,16,128]{2,1,0:T(8,128)}), f32[16,16,128]{2,1,0:T(8,128)S(1)}, u32[]{:S(2)}, u32[]{:S(2)}) async-start(f32[16,16,128]{2,1,0:T(8,128)} %broadcast_in_dim.28), calls=%async_computation.2 | async-start | bytes 262144 | tf_op jit(solution)/shard_map/all_to_all | solution.py:25
  141.0 0.7 fusion.5
  141.6 3.6 %all-gather.6 = f32[128,1024]{1,0:T(8,128)S(1)} all-gather(f32[64,1024]{1,0:T(8,128)S(1)} %fusion.5), channel_id=8, replica_groups={{0,1},{3,2},{4,5},{7,6},{8,9},{11,10},{12,13},{15,14},{17,16},{18,19},{..., dimensions={0}, use_global_device_ids=true | all-gather | bytes 786432 | tf_op jit(solution)/shard_map/all_gather | solution.py:277
  145.2 0.3 reshape.64
  145.5 1.9 %copy.29 = f32[64,64,2,16]{1,3,2,0:T(8,128)} copy(f32[64,64,2,16]{0,3,1,2:T(8,128)S(1)} %bitcast.41) | data formatting | bytes 1048576 | tf_op jit(solution)/shard_map/transpose | solution.py:281
  147.4 0.6 broadcast_multiply_fusion
  148.0 4.6 %all-to-all-done.2 = f32[16,16,128]{2,1,0:T(8,128)S(1)} async-done(((f32[16,16,128]{2,1,0:T(8,128)}), f32[16,16,128]{2,1,0:T(8,128)S(1)}, u32[]{:S(2)}, u32[]{:S(2)}) %all-to-all-start.2) | async-done | bytes 131104 | tf_op jit(solution)/shard_map/all_to_all | solution.py:25
  152.6 8.6 %all-gather.5 = f32[64,128]{1,0:T(8,128)S(1)} all-gather(f32[16,128]{1,0:T(8,128)S(1)} %reduce_sum.39), channel_id=7, replica_groups={{0,1,2,3},{4,5,6,7},{8,9,10,11},{12,13,14,15},{16,17,18,19},{20,21,22,2..., dimensions={0}, use_global_device_ids=true | all-gather | bytes 40960 | tf_op jit(solution)/shard_map/all_gather | solution.py:270
  161.2 2.0 %shard_map.79 = f32[32,128]{1,0:T(8,128)} custom-call(f32[2,2,16,128]{3,2,1,0:T(8,128)S(1)} %bitcast.40), custom_call_target="tpu_custom_call" | custom-call | tf_op jit(solution)/shard_map/pallas_call | solution.py:62
  (14 shorter events, 0.1 us)
Async XLA Ops:
  0.6 0.9 copy-start
  0.6 0.8 copy-start.2
  0.7 0.9 copy-start.1
  137.0 15.6 %all-to-all-start.2 = ((f32[16,16,128]{2,1,0:T(8,128)}), f32[16,16,128]{2,1,0:T(8,128)S(1)}, u32[]{:S(2)}, u32[]{:S(2)}) async-start(f32[16,16,128]{2,1,0:T(8,128)} %broadcast_in_dim.28), calls=%async_computation.2 | async-start | bytes 262144 | tf_op jit(solution)/shard_map/all_to_all | solution.py:25

commit v8 on v7

--- a/solution.py
+++ b/solution.py
@@ -36,8 +36,30 @@
     return lax.dot_general(left, right, (((1,), (1,)), ((), ())), precision=exact_mode)
 
 
-def mul_tn(left, right):
-    return lax.dot_general(left, right, (((0,), (0,)), ((), ())), precision=exact_mode)
+def head_and_rest(matrix):
+    head = matrix.astype(jnp.bfloat16)
+    return head, (matrix - head.astype(jnp.float32)).astype(jnp.bfloat16)
+
+
+def three_products(left, right, contract):
+    left_head, left_rest = head_and_rest(left)
+    right_head, right_rest = head_and_rest(right)
+
+    def product(one, other):
+        return lax.dot_general(
+            one, other, (contract, ((), ())), preferred_element_type=jnp.float32
+        )
+
+    small = product(left_head, right_rest) + product(left_rest, right_head)
+    return product(left_head, right_head) + small
+
+
+def times(left, right):
+    return three_products(left, right, ((1,), (0,)))
+
+
+def gram_of(z):
+    return three_products(z, z, ((1,), (1,)))
 
 
 def orth_factor(gram):
@@ -49,9 +71,9 @@
     factor = None
     for step in range(NEWTON):
         move = 1.5 * identity - 0.5 * gram
-        factor = move if factor is None else mul(factor, move)
+        factor = move if factor is None else times(factor, move)
         if step + 1 < NEWTON:
-            gram = mul(mul(move, gram), move)
+            gram = times(times(move, gram), move)
     return factor / jnp.sqrt(total)
 
 
@@ -93,7 +115,7 @@
 
 def to_second(size_one, slices, z_parts, got, one, projected):
     z = jnp.sum(z_parts[...], axis=0)
-    new = mul(orth_factor(mul_nt(z, z)), z)
+    new = times(orth_factor(gram_of(z)), z)
     one[...] = new
     rank = new.shape[0]
     width = got.shape[2]
@@ -108,7 +130,7 @@
 
 def to_third(z_parts, projected, one, two, one_own, two_own, spread):
     z = jnp.sum(z_parts[...], axis=0)
-    new = mul(orth_factor(mul_nt(z, z)), z)
+    new = times(orth_factor(gram_of(z)), z)
     two[...] = new
     rank, length_one = one.shape
     length_two = new.shape[1]
@@ -134,11 +156,11 @@
         jnp.concatenate([parts[share, level] for share in range(shares)], axis=0)
         for level in range(parts.shape[1])
     ]
-    gram = functools.reduce(jnp.add, [mul_nt(z, z) for z in whole])
+    gram = functools.reduce(jnp.add, [gram_of(z) for z in whole])
     own = whole[0]
     for level in range(1, len(whole)):
         own = jnp.where(lax.axis_index("depth") == level, whole[level], own)
-    three[...] = mul(orth_factor(gram), own) * scale
+    three[...] = times(orth_factor(gram), own) * scale
 
 
 def own_rows(axis, size, length):

time: 164 us -> 163 us (level)
  no operation moved by 1% of the time
where the time goes in v8:
time: 163 us; the launch traced here: 162 us
  blocking collectives  139 us (85%)
  Pallas kernels  7.44 us (5%)
  waiting for transfers between devices  4.62 us (3%)
  local copies, waits for them, and re-layouts  4.32 us (3%)
  starting transfers between devices  3.95 us (2%)
    all_to_all x1, blocking collectives, body(): lax.all_to_all(shard, EVERYWHERE, 0, 0, tiled=True, axis_index_groups=blo...  53.1 us
    all_gather x1, blocking collectives, body(): lax.all_gather(jnp.concatenate([own, one_packed], axis=0), ('rows', 'dept...  32.4 us
    all_gather x1, blocking collectives, body(): lax.all_gather(projected, ('cols', 'depth'), axis_index_groups=teams)  15.3 us
    all_to_all x1, blocking collectives, body(): lax.all_to_all(shard, 'cols', 0, 0, tiled=True)  9.55 us
    all_gather x1, blocking collectives, body(): z_parts = lax.all_gather(z_part, ('cols', 'depth'), axis_index_groups=near)  8.59 us
    pallas_call x5, Pallas kernels, kernel_call(): pl.pallas_call(kernel, out_shape=outs[0] if one else outs, in_specs=[whol...  7.44 us
    all_gather x1, blocking collectives, body(): z_parts = lax.all_gather(z_part, 'cols', axis_index_groups=far)  6.88 us
    all_gather x1, blocking collectives, body(): lax.all_gather(z_part, ('cols', 'depth'), axis_index_groups=near)  6.07 us
  transfers between devices with their start and end apart: 1, of which 1 were waited for; matrix products, arithmetic and copies ran while one was open for 2% of the time, Pallas kernels for 0%

profile of v8, /device:TPU:65, one launch (start us, length us, event | category | flops | bytes accessed | tf_op | source)
XLA Modules:
  0.0 162.4 jit_solution(10714204846674007092)
XLA Ops:
  0.6 0.0 copy-start
  0.6 0.0 copy-start.2
  0.7 0.0 copy-start.1
  0.7 0.8 fusion.2
  1.4 0.0 copy-done.2
  1.4 0.1 copy-done
  1.6 0.0 copy-done.1
  1.6 0.2 fusion.4
  1.8 0.1 pad_maximum_fusion.4
  1.9 0.1 pad_maximum_fusion.3
  2.0 53.1 %all_to_all.15 = f32[16,16,128]{2,1,0:T(8,128)S(1)} all-to-all(f32[16,16,128]{2,1,0:T(8,128)S(1)} %pad_maximum_fusion), channel_id=1, replica_groups={{0,1,3,2,4,5,7,6,8,9,11,10,12,13,15,14},{17,16,18,19,21,20,22,23,25,24,..., dimensions={0} | all-to-all | bytes 262144 | tf_op jit(solution)/shard_map/all_to_all | solution.py:234
  55.1 0.1 slice_bitcast_fusion.1
  55.2 0.1 copy.26
  55.3 0.1 reshape.58
  55.5 0.1 copy.25
  55.6 0.1 pad_maximum_fusion.1
  55.7 0.1 copy.27
  55.7 32.4 %all-gather = f32[1152,128]{1,0:T(8,128)S(1)} all-gather(f32[72,128]{1,0:T(8,128)S(1)} %copy.27), channel_id=2, replica_groups={{0,17,32,49,64,81,96,113,128,145,160,177,192,209,224,241},{1,16,33,48,6..., dimensions={0}, use_global_device_ids=true | all-gather | bytes 626688 | tf_op jit(solution)/shard_map/all_gather | solution.py:244
  88.2 1.5 shard_map.75
  89.6 6.1 %all-gather.1 = f32[256,256]{1,0:T(8,128)S(1)} all-gather(f32[64,256]{1,0:T(8,128)S(1)} %shard_map.75), channel_id=3, replica_groups={{0,1,2,3},{4,5,6,7},{8,9,10,11},{12,13,14,15},{16,17,18,19},{20,21,22,2..., dimensions={0}, use_global_device_ids=true | all-gather | bytes 327680 | tf_op jit(solution)/shard_map/all_gather | solution.py:254
  95.7 6.9 %all-gather.2 = f32[128,256]{1,0:T(8,128)S(1)} all-gather(f32[64,256]{1,0:T(8,128)S(1)} %reduce_sum.37), channel_id=4, replica_groups={{0,4},{2,6},{8,12},{10,14},{1,5},{3,7},{9,13},{11,15},{16,20},{18,22},{..., dimensions={0}, use_global_device_ids=true | all-gather | bytes 196608 | tf_op jit(solution)/shard_map/all_gather | solution.py:255
  102.6 1.5 shard_map.76
  104.1 15.3 %all-gather.3.projected = f32[1024,128]{1,0:T(8,128)S(1)} all-gather(f32[256,128]{1,0:T(8,128)S(1)} %get-tuple-element.31), channel_id=5, replica_groups={{0,3,4,7},{1,2,5,6},{8,11,12,15},{9,10,13,14},{16,19,20,23},{17,18,21,2..., dimensions={0}, use_global_device_ids=true | all-gather | bytes 655360 | tf_op jit(solution)/shard_map/all_gather | solution.py:263
  119.4 0.9 shard_map.77
  120.4 1.9 %all-gather.4 = f32[128,128]{1,0:T(8,128)S(1)} all-gather(f32[64,128]{1,0:T(8,128)S(1)} %shard_map.77), channel_id=6, replica_groups=mesh['groups'=2,'rows'=16,'cols'=8,'depth'=2] {'depth'}, dimensions={0}, use_global_device_ids=true | all-gather | bytes 98304 | tf_op jit(solution)/shard_map/all_gather | solution.py:266
  122.3 1.8 %shard_map.78 = (f32[64,128]{1,0:T(8,128)S(1)}, f32[16,64]{1,0:T(8,128)S(1)}, f32[16,64]{1,0:T(8,128)S(1)}, f32[256,16]{1,0:T(8,128)S(1)}) custom-call(f32[2,64,128]{2,1,0:T(8,128)S(1)} %bitcast.39, f32[1024,128]{1,0:T(8,128)S(1)} %all-gather.3.projected, f32[64,256]{1,0:T(8,128)S(1)} %get-tuple-element.32.one), custom_call_target="tpu_custom_call" | custom-call | tf_op jit(solution)/shard_map/pallas_call | solution.py:84
  124.1 0.1 all_gather_reshape.3
  124.2 1.9 %all_gather.55 = f32[2,16,256]{2,1,0:T(8,128)S(1)} all-gather(f32[1,16,256]{2,1,0:T(8,128)S(1)} %all_gather_reshape.3), channel_id=1, replica_groups={{0,1},{3,2},{4,5},{7,6},{8,9},{11,10},{12,13},{15,14},{17,16},{18,19},{..., dimensions={0}, use_global_device_ids=true | all-gather | bytes 49152 | tf_op jit(solution)/shard_map/all_gather | solution.py:281
  126.1 0.2 fusion
  126.3 9.5 %all_to_all.16 = f32[8,16,128]{2,1,0:T(8,128)S(1)} all-to-all(f32[8,16,128]{2,1,0:T(8,128)S(1)} %bitcast.48), channel_id=1, replica_groups=mesh['groups'=2,'rows'=16,'cols'=8,'depth'=2] {'cols'}, dimensions={0} | all-to-all | bytes 131072 | tf_op jit(solution)/shard_map/all_to_all | solution.py:288
  135.9 0.6 broadcast_in_dim.28
  136.5 4.0 %all-to-all-start.2 = ((f32[16,16,128]{2,1,0:T(8,128)}), f32[16,16,128]{2,1,0:T(8,128)S(1)}, u32[]{:S(2)}, u32[]{:S(2)}) async-start(f32[16,16,128]{2,1,0:T(8,128)} %broadcast_in_dim.28), calls=%async_computation.2 | async-start | bytes 262144 | tf_op jit(solution)/shard_map/all_to_all | solution.py:25
  140.5 0.7 fusion.5
  141.2 3.6 %all-gather.6 = f32[128,1024]{1,0:T(8,128)S(1)} all-gather(f32[64,1024]{1,0:T(8,128)S(1)} %fusion.5), channel_id=8, replica_groups={{0,1},{3,2},{4,5},{7,6},{8,9},{11,10},{12,13},{15,14},{17,16},{18,19},{..., dimensions={0}, use_global_device_ids=true | all-gather | bytes 786432 | tf_op jit(solution)/shard_map/all_gather | solution.py:299
  144.7 0.3 reshape.64
  145.0 1.9 %copy.29 = f32[64,64,2,16]{1,3,2,0:T(8,128)} copy(f32[64,64,2,16]{0,3,1,2:T(8,128)S(1)} %bitcast.41) | data formatting | bytes 1048576 | tf_op jit(solution)/shard_map/transpose | solution.py:303
  146.9 0.6 broadcast_multiply_fusion
  147.5 4.6 %all-to-all-done.2 = f32[16,16,128]{2,1,0:T(8,128)S(1)} async-done(((f32[16,16,128]{2,1,0:T(8,128)}), f32[16,16,128]{2,1,0:T(8,128)S(1)}, u32[]{:S(2)}, u32[]{:S(2)}) %all-to-all-start.2) | async-done | bytes 131104 | tf_op jit(solution)/shard_map/all_to_all | solution.py:25
  152.1 8.6 %all-gather.5 = f32[64,128]{1,0:T(8,128)S(1)} all-gather(f32[16,128]{1,0:T(8,128)S(1)} %reduce_sum.39), channel_id=7, replica_groups={{0,1,2,3},{4,5,6,7},{8,9,10,11},{12,13,14,15},{16,17,18,19},{20,21,22,2..., dimensions={0}, use_global_device_ids=true | all-gather | bytes 40960 | tf_op jit(solution)/shard_map/all_gather | solution.py:292
  160.7 1.7 %shard_map.79 = f32[32,128]{1,0:T(8,128)} custom-call(f32[2,2,16,128]{3,2,1,0:T(8,128)S(1)} %bitcast.40), custom_call_target="tpu_custom_call" | custom-call | tf_op jit(solution)/shard_map/pallas_call | solution.py:84
  (14 shorter events, 0.1 us)
Async XLA Ops:
  0.6 0.9 copy-start
  0.6 0.8 copy-start.2
  0.7 0.9 copy-start.1
  136.5 15.6 %all-to-all-start.2 = ((f32[16,16,128]{2,1,0:T(8,128)}), f32[16,16,128]{2,1,0:T(8,128)S(1)}, u32[]{:S(2)}, u32[]{:S(2)}) async-start(f32[16,16,128]{2,1,0:T(8,128)} %broadcast_in_dim.28), calls=%async_computation.2 | async-start | bytes 262144 | tf_op jit(solution)/shard_map/all_to_all | solution.py:25

commit v9 on v7

--- a/solution.py
+++ b/solution.py
@@ -259,32 +259,41 @@
     spread = lax.all_gather(spread.reshape(half, -1), EVERYWHERE, axis_index_groups=chips)
     spread = spread.reshape(rank_three, -1)
     shares = jnp.broadcast_to(
-        mul(spread, flat).reshape(1, half_team, -1, size_three),
-        (cols // half_team, half_team, rank_three // half_team, size_three),
+        mul(spread, flat).reshape(1, CLASSES, -1, size_three),
+        (cols // CLASSES, CLASSES, rank_three // CLASSES, size_three),
     ).reshape(cols, -1, size_three)
     z_part, two, projected, one_own, two_own = alone(
         lambda shard: lax.all_to_all(shard, "cols", 0, 0, tiled=True),
         shares, two, projected, one_own, two_own,
     )
     z_part = from_everyone(z_part.sum(axis=0), "rows").sum(axis=0)
-    z_parts = lax.all_gather(z_part, ("cols", "depth"), axis_index_groups=near)
+    core = lax.all_gather(
+        mul(two, projected.T), EVERYWHERE, axis_index_groups=chips
+    )
+    core = core.reshape(depth, rank_two, -1, rank_one)
+    core = core.transpose(3, 1, 0, 2).reshape(rank_one, rank_two, rank_three)
+    one_own = one_own * math.sqrt(length_one)
+    two_own = two_own * math.sqrt(length_two)
+    z_parts, core, one_own, two_own = alone(
+        lambda shard: lax.all_to_all(
+            jnp.broadcast_to(shard[None], (CLASSES * depth, *shard.shape)),
+            ("cols", "depth"),
+            0,
+            0,
+            tiled=True,
+            axis_index_groups=[
+                list(range(first, first + CLASSES * depth))
+                for first in range(0, cols * depth, CLASSES * depth)
+            ],
+        ),
+        z_part, core, one_own, two_own,
+    )
     three = kernel_call(
         functools.partial(last_orth, math.sqrt(length_three)),
         (rank_three, size_three),
-        z_parts.reshape(half_team, depth, -1, size_three),
-    )
-
-    core = lax.all_gather(
-        mul(two, projected.T), EVERYWHERE, axis_index_groups=chips
-    )
-    core = core.reshape(depth, rank_two, -1, rank_one)
-    core = core.transpose(3, 1, 0, 2).reshape(rank_one, rank_two, rank_three)
-    return (
-        one_own * math.sqrt(length_one),
-        two_own * math.sqrt(length_two),
-        three.T,
-        core,
-    )
+        z_parts.reshape(CLASSES, depth, -1, size_three),
+    )
+    return one_own, two_own, three.T, core
 
 
 def solution(mesh):

time: 164 us -> 164 us (level)
    all_to_all x0 -> x1, blocking collectives: none -> 10.1 us  [body(): lax.all_to_all(jnp.broadcast_to(shard[None], (CLASSES * depth, *shard.sha...]
    all_gather x1 -> x0, blocking collectives: 8.59 us -> none  [body(): z_parts = lax.all_gather(z_part, ('cols', 'depth'), axis_index_groups=near)]
where the time goes in v9:
time: 164 us
  blocking collectives  140 us (85%)
  Pallas kernels  8.15 us (5%)
  waiting for transfers between devices  4.41 us (3%)
  local copies, waits for them, and re-layouts  4.31 us (3%)
  starting transfers between devices  3.94 us (2%)
    all_to_all x1, blocking collectives, body(): lax.all_to_all(shard, EVERYWHERE, 0, 0, tiled=True, axis_index_groups=blo...  53.1 us
    all_gather x1, blocking collectives, body(): lax.all_gather(jnp.concatenate([own, one_packed], axis=0), ('rows', 'dept...  32.4 us
    all_gather x1, blocking collectives, body(): lax.all_gather(projected, ('cols', 'depth'), axis_index_groups=teams)  15.3 us
    all_to_all x1, blocking collectives, body(): lax.all_to_all(jnp.broadcast_to(shard[None], (CLASSES * depth, *shard.sha...  10.1 us
    all_to_all x1, blocking collectives, body(): lax.all_to_all(shard, 'cols', 0, 0, tiled=True)  9.31 us
    pallas_call x5, Pallas kernels, kernel_call(): pl.pallas_call(kernel, out_shape=outs[0] if one else outs, in_specs=[whol...  8.15 us
    all_gather x1, blocking collectives, body(): z_parts = lax.all_gather(z_part, 'cols', axis_index_groups=far)  6.88 us
    all_gather x1, blocking collectives, body(): lax.all_gather(z_part, ('cols', 'depth'), axis_index_groups=near)  6.07 us
  transfers between devices with their start and end apart: 1, of which 1 were waited for; matrix products, arithmetic and copies ran while one was open for 2% of the time, Pallas kernels for 0%

profile of v9, /device:TPU:65, one launch (start us, length us, event | category | flops | bytes accessed | tf_op | source)
XLA Modules:
  0.0 164.0 jit_solution(334055909300721964)
XLA Ops:
  0.6 0.0 copy-start
  0.6 0.0 copy-start.2
  0.7 0.0 copy-start.1
  0.7 0.8 fusion.2
  1.4 0.0 copy-done.2
  1.4 0.1 copy-done
  1.6 0.0 copy-done.1
  1.6 0.2 fusion.4
  1.8 0.1 pad_maximum_fusion.4
  1.9 0.1 pad_maximum_fusion.3
  2.0 53.1 %all_to_all.20 = f32[16,16,128]{2,1,0:T(8,128)S(1)} all-to-all(f32[16,16,128]{2,1,0:T(8,128)S(1)} %pad_maximum_fusion), channel_id=1, replica_groups={{0,1,3,2,4,5,7,6,8,9,11,10,12,13,15,14},{17,16,18,19,21,20,22,23,25,24,..., dimensions={0} | all-to-all | bytes 262144 | tf_op jit(solution)/shard_map/all_to_all | solution.py:212
  55.1 0.1 slice_bitcast_fusion.1
  55.2 0.1 copy.26
  55.3 0.1 reshape.61
  55.5 0.1 copy.25
  55.6 0.1 pad_maximum_fusion.1
  55.7 0.1 copy.27
  55.7 32.4 %all-gather = f32[1152,128]{1,0:T(8,128)S(1)} all-gather(f32[72,128]{1,0:T(8,128)S(1)} %copy.27), channel_id=2, replica_groups={{0,17,32,49,64,81,96,113,128,145,160,177,192,209,224,241},{1,16,33,48,6..., dimensions={0}, use_global_device_ids=true | all-gather | bytes 626688 | tf_op jit(solution)/shard_map/all_gather | solution.py:222
  88.2 1.5 shard_map.75
  89.6 6.1 %all-gather.1 = f32[256,256]{1,0:T(8,128)S(1)} all-gather(f32[64,256]{1,0:T(8,128)S(1)} %shard_map.75), channel_id=3, replica_groups={{0,1,2,3},{4,5,6,7},{8,9,10,11},{12,13,14,15},{16,17,18,19},{20,21,22,2..., dimensions={0}, use_global_device_ids=true | all-gather | bytes 327680 | tf_op jit(solution)/shard_map/all_gather | solution.py:232
  95.7 6.9 %all-gather.2 = f32[128,256]{1,0:T(8,128)S(1)} all-gather(f32[64,256]{1,0:T(8,128)S(1)} %reduce_sum.37), channel_id=4, replica_groups={{0,4},{2,6},{8,12},{10,14},{1,5},{3,7},{9,13},{11,15},{16,20},{18,22},{..., dimensions={0}, use_global_device_ids=true | all-gather | bytes 196608 | tf_op jit(solution)/shard_map/all_gather | solution.py:233
  102.6 1.8 %shard_map.76 = (f32[64,256]{1,0:T(8,128)S(1)}, f32[256,128]{1,0:T(8,128)S(1)}) custom-call(f32[2,64,256]{2,1,0:T(8,128)S(1)} %bitcast.39, f32[16,72,128]{2,1,0:T(8,128)S(1)} %bitcast.36), custom_call_target="tpu_custom_call" | custom-call | tf_op jit(solution)/shard_map/pallas_call | solution.py:62
  104.4 15.3 %all-gather.3.projected = f32[1024,128]{1,0:T(8,128)S(1)} all-gather(f32[256,128]{1,0:T(8,128)S(1)} %get-tuple-element.39), channel_id=5, replica_groups={{0,3,4,7},{1,2,5,6},{8,11,12,15},{9,10,13,14},{16,19,20,23},{17,18,21,2..., dimensions={0}, use_global_device_ids=true | all-gather | bytes 655360 | tf_op jit(solution)/shard_map/all_gather | solution.py:241
  119.7 0.9 shard_map.77
  120.6 1.9 %all-gather.4 = f32[128,128]{1,0:T(8,128)S(1)} all-gather(f32[64,128]{1,0:T(8,128)S(1)} %shard_map.77), channel_id=6, replica_groups=mesh['groups'=2,'rows'=16,'cols'=8,'depth'=2] {'depth'}, dimensions={0}, use_global_device_ids=true | all-gather | bytes 98304 | tf_op jit(solution)/shard_map/all_gather | solution.py:244
  122.6 2.0 %shard_map.78 = (f32[64,128]{1,0:T(8,128)S(1)}, f32[16,64]{1,0:T(8,128)S(1)}, f32[16,64]{1,0:T(8,128)S(1)}, f32[256,16]{1,0:T(8,128)S(1)}) custom-call(f32[2,64,128]{2,1,0:T(8,128)S(1)} %bitcast.40, f32[1024,128]{1,0:T(8,128)S(1)} %all-gather.3.projected, f32[64,256]{1,0:T(8,128)S(1)} %get-tuple-element.40.one), custom_call_target="tpu_custom_call" | custom-call | tf_op jit(solution)/shard_map/pallas_call | solution.py:62
  124.6 0.1 all_gather_reshape.3
  124.7 1.9 %all_gather.49 = f32[2,16,256]{2,1,0:T(8,128)S(1)} all-gather(f32[1,16,256]{2,1,0:T(8,128)S(1)} %all_gather_reshape.3), channel_id=1, replica_groups={{0,1},{3,2},{4,5},{7,6},{8,9},{11,10},{12,13},{15,14},{17,16},{18,19},{..., dimensions={0}, use_global_device_ids=true | all-gather | bytes 49152 | tf_op jit(solution)/shard_map/all_gather | solution.py:259
  126.6 0.2 fusion
  126.8 9.3 %all_to_all.21 = f32[8,8,128]{2,1,0:T(8,128)S(1)} all-to-all(f32[8,8,128]{2,1,0:T(8,128)S(1)} %bitcast.51), channel_id=1, replica_groups=mesh['groups'=2,'rows'=16,'cols'=8,'depth'=2] {'cols'}, dimensions={0} | all-to-all | bytes 65536 | tf_op jit(solution)/shard_map/all_to_all | solution.py:266
  136.1 0.6 broadcast_in_dim.16
  136.7 3.9 %all-to-all-start.2 = ((f32[16,8,128]{2,1,0:T(8,128)}), f32[16,8,128]{2,1,0:T(8,128)S(1)}, u32[]{:S(2)}, u32[]{:S(2)}) async-start(f32[16,8,128]{2,1,0:T(8,128)} %broadcast_in_dim.16), calls=%async_computation.2 | async-start | bytes 131072 | tf_op jit(solution)/shard_map/all_to_all | solution.py:25
  140.7 0.7 fusion.5
  141.3 3.5 %all-gather.5 = f32[128,1024]{1,0:T(8,128)S(1)} all-gather(f32[64,1024]{1,0:T(8,128)S(1)} %fusion.5), channel_id=7, replica_groups={{0,1},{3,2},{4,5},{7,6},{8,9},{11,10},{12,13},{15,14},{17,16},{18,19},{..., dimensions={0}, use_global_device_ids=true | all-gather | bytes 786432 | tf_op jit(solution)/shard_map/all_gather | solution.py:270
  144.8 0.3 reshape.67
  145.1 1.9 %copy.29 = f32[64,64,2,16]{1,3,2,0:T(8,128)} copy(f32[64,64,2,16]{0,3,1,2:T(8,128)S(1)} %bitcast.42) | data formatting | bytes 1048576 | tf_op jit(solution)/shard_map/transpose | solution.py:274
  147.0 0.6 broadcast_multiply_fusion
  147.6 4.4 %all-to-all-done.2 = f32[16,8,128]{2,1,0:T(8,128)S(1)} async-done(((f32[16,8,128]{2,1,0:T(8,128)}), f32[16,8,128]{2,1,0:T(8,128)S(1)}, u32[]{:S(2)}, u32[]{:S(2)}) %all-to-all-start.2) | async-done | bytes 65568 | tf_op jit(solution)/shard_map/all_to_all | solution.py:25
  152.0 10.1 %all_to_all.22 = f32[8,8,128]{2,1,0:T(8,128)S(1)} all-to-all(f32[8,8,128]{2,1,0:T(8,128)S(1)} %broadcast_in_dim.17), channel_id=1, replica_groups={{0,1,2,3,4,5,6,7},{8,9,10,11,12,13,14,15},{16,17,18,19,20,21,22,23},{24..., dimensions={0} | all-to-all | bytes 65536 | tf_op jit(solution)/shard_map/all_to_all | solution.py:278
  162.1 2.0 %shard_map.79 = f32[32,128]{1,0:T(8,128)} custom-call(f32[4,2,8,128]{3,2,1,0:T(8,128)S(1)} %bitcast.41), custom_call_target="tpu_custom_call" | custom-call | tf_op jit(solution)/shard_map/pallas_call | solution.py:62
  (15 shorter events, 0.1 us)
Async XLA Ops:
  0.6 0.9 copy-start
  0.6 0.8 copy-start.2
  0.7 0.9 copy-start.1
  136.7 15.2 %all-to-all-start.2 = ((f32[16,8,128]{2,1,0:T(8,128)}), f32[16,8,128]{2,1,0:T(8,128)S(1)}, u32[]{:S(2)}, u32[]{:S(2)}) async-start(f32[16,8,128]{2,1,0:T(8,128)} %broadcast_in_dim.16), calls=%async_computation.2 | async-start | bytes 131072 | tf_op jit(solution)/shard_map/all_to_all | solution.py:25

commit v10 on v7

--- a/solution.py
+++ b/solution.py
@@ -188,11 +188,10 @@
         list(range(first * depth, (first + half_team) * depth))
         for first in range(0, cols, half_team)
     ]
-    far = [
-        [first + at, first + half_team + at]
-        for first in range(0, cols, CLASSES)
-        for at in range(half_team)
-    ]
+    far = []
+    for last in range(half_team - 1, cols, half_team):
+        pair = [last, (last + 1) % cols]
+        far.append(pair if last % CLASSES < half_team else pair[::-1])
     slices = rank_three // (CLASSES * depth)
     flat = tensor.reshape(size_one * size_two, size_three)
 

time: 164 us -> 162 us (0.988)
  no operation moved by 1% of the time
where the time goes in v10:
time: 162 us
  blocking collectives  138 us (85%)
  Pallas kernels  8.15 us (5%)
  waiting for transfers between devices  4.64 us (3%)
  local copies, waits for them, and re-layouts  4.32 us (3%)
  starting transfers between devices  3.95 us (2%)
    all_to_all x1, blocking collectives, body(): lax.all_to_all(shard, EVERYWHERE, 0, 0, tiled=True, axis_index_groups=blo...  53.1 us
    all_gather x1, blocking collectives, body(): lax.all_gather(jnp.concatenate([own, one_packed], axis=0), ('rows', 'dept...  32.4 us
    all_gather x1, blocking collectives, body(): lax.all_gather(projected, ('cols', 'depth'), axis_index_groups=teams)  15.1 us
    all_to_all x1, blocking collectives, body(): lax.all_to_all(shard, 'cols', 0, 0, tiled=True)  9.54 us
    all_gather x1, blocking collectives, body(): z_parts = lax.all_gather(z_part, ('cols', 'depth'), axis_index_groups=near)  8.59 us
    pallas_call x5, Pallas kernels, kernel_call(): pl.pallas_call(kernel, out_shape=outs[0] if one else outs, in_specs=[whol...  8.15 us
    all_gather x1, blocking collectives, body(): lax.all_gather(z_part, ('cols', 'depth'), axis_index_groups=near)  6.07 us
    all_gather x1, blocking collectives, body(): z_parts = lax.all_gather(z_part, 'cols', axis_index_groups=far)  5.39 us
  transfers between devices with their start and end apart: 1, of which 1 were waited for; matrix products, arithmetic and copies ran while one was open for 2% of the time, Pallas kernels for 0%

profile of v10, /device:TPU:65, one launch (start us, length us, event | category | flops | bytes accessed | tf_op | source)
XLA Modules:
  0.0 162.0 jit_solution(15692501706879700731)
XLA Ops:
  0.6 0.0 copy-start
  0.6 0.0 copy-start.2
  0.7 0.0 copy-start.1
  0.7 0.8 fusion.2
  1.4 0.0 copy-done.2
  1.4 0.1 copy-done
  1.6 0.0 copy-done.1
  1.6 0.2 fusion.4
  1.8 0.1 pad_maximum_fusion.4
  1.9 0.1 pad_maximum_fusion.3
  2.0 53.1 %all_to_all.15 = f32[16,16,128]{2,1,0:T(8,128)S(1)} all-to-all(f32[16,16,128]{2,1,0:T(8,128)S(1)} %pad_maximum_fusion), channel_id=1, replica_groups={{0,1,3,2,4,5,7,6,8,9,11,10,12,13,15,14},{17,16,18,19,21,20,22,23,25,24,..., dimensions={0} | all-to-all | bytes 262144 | tf_op jit(solution)/shard_map/all_to_all | solution.py:211
  55.1 0.1 slice_bitcast_fusion.1
  55.2 0.1 copy.26
  55.3 0.1 reshape.58
  55.5 0.1 copy.25
  55.6 0.1 pad_maximum_fusion.1
  55.7 0.1 copy.27
  55.7 32.4 %all-gather = f32[1152,128]{1,0:T(8,128)S(1)} all-gather(f32[72,128]{1,0:T(8,128)S(1)} %copy.27), channel_id=2, replica_groups={{0,17,32,49,64,81,96,113,128,145,160,177,192,209,224,241},{1,16,33,48,6..., dimensions={0}, use_global_device_ids=true | all-gather | bytes 626688 | tf_op jit(solution)/shard_map/all_gather | solution.py:221
  88.2 1.5 shard_map.75
  89.6 6.1 %all-gather.1 = f32[256,256]{1,0:T(8,128)S(1)} all-gather(f32[64,256]{1,0:T(8,128)S(1)} %shard_map.75), channel_id=3, replica_groups={{0,1,2,3},{4,5,6,7},{8,9,10,11},{12,13,14,15},{16,17,18,19},{20,21,22,2..., dimensions={0}, use_global_device_ids=true | all-gather | bytes 327680 | tf_op jit(solution)/shard_map/all_gather | solution.py:231
  95.7 5.4 %all-gather.2 = f32[128,256]{1,0:T(8,128)S(1)} all-gather(f32[64,256]{1,0:T(8,128)S(1)} %reduce_sum.37), channel_id=4, replica_groups={{2,4},{8,6},{10,12},{0,14},{3,5},{9,7},{11,13},{1,15},{18,20},{24,22},{..., dimensions={0}, use_global_device_ids=true | all-gather | bytes 196608 | tf_op jit(solution)/shard_map/all_gather | solution.py:232
  101.1 1.8 %shard_map.76 = (f32[64,256]{1,0:T(8,128)S(1)}, f32[256,128]{1,0:T(8,128)S(1)}) custom-call(f32[2,64,256]{2,1,0:T(8,128)S(1)} %bitcast.38, f32[16,72,128]{2,1,0:T(8,128)S(1)} %bitcast.35), custom_call_target="tpu_custom_call" | custom-call | tf_op jit(solution)/shard_map/pallas_call | solution.py:62
  102.9 15.1 %all-gather.3.projected = f32[1024,128]{1,0:T(8,128)S(1)} all-gather(f32[256,128]{1,0:T(8,128)S(1)} %get-tuple-element.31), channel_id=5, replica_groups={{0,3,4,7},{1,2,5,6},{8,11,12,15},{9,10,13,14},{16,19,20,23},{17,18,21,2..., dimensions={0}, use_global_device_ids=true | all-gather | bytes 655360 | tf_op jit(solution)/shard_map/all_gather | solution.py:240
  118.0 0.9 shard_map.77
  119.0 2.5 %all-gather.4 = f32[128,128]{1,0:T(8,128)S(1)} all-gather(f32[64,128]{1,0:T(8,128)S(1)} %shard_map.77), channel_id=6, replica_groups=mesh['groups'=2,'rows'=16,'cols'=8,'depth'=2] {'depth'}, dimensions={0}, use_global_device_ids=true | all-gather | bytes 98304 | tf_op jit(solution)/shard_map/all_gather | solution.py:243
  121.5 2.0 %shard_map.78 = (f32[64,128]{1,0:T(8,128)S(1)}, f32[16,64]{1,0:T(8,128)S(1)}, f32[16,64]{1,0:T(8,128)S(1)}, f32[256,16]{1,0:T(8,128)S(1)}) custom-call(f32[2,64,128]{2,1,0:T(8,128)S(1)} %bitcast.39, f32[1024,128]{1,0:T(8,128)S(1)} %all-gather.3.projected, f32[64,256]{1,0:T(8,128)S(1)} %get-tuple-element.32.one), custom_call_target="tpu_custom_call" | custom-call | tf_op jit(solution)/shard_map/pallas_call | solution.py:62
  123.5 0.1 all_gather_reshape.3
  123.6 1.9 %all_gather.55 = f32[2,16,256]{2,1,0:T(8,128)S(1)} all-gather(f32[1,16,256]{2,1,0:T(8,128)S(1)} %all_gather_reshape.3), channel_id=1, replica_groups={{0,1},{3,2},{4,5},{7,6},{8,9},{11,10},{12,13},{15,14},{17,16},{18,19},{..., dimensions={0}, use_global_device_ids=true | all-gather | bytes 49152 | tf_op jit(solution)/shard_map/all_gather | solution.py:258
  125.5 0.2 fusion
  125.7 9.5 %all_to_all.16 = f32[8,16,128]{2,1,0:T(8,128)S(1)} all-to-all(f32[8,16,128]{2,1,0:T(8,128)S(1)} %bitcast.48), channel_id=1, replica_groups=mesh['groups'=2,'rows'=16,'cols'=8,'depth'=2] {'cols'}, dimensions={0} | all-to-all | bytes 131072 | tf_op jit(solution)/shard_map/all_to_all | solution.py:265
  135.3 0.6 broadcast_in_dim.28
  135.9 4.0 %all-to-all-start.2 = ((f32[16,16,128]{2,1,0:T(8,128)}), f32[16,16,128]{2,1,0:T(8,128)S(1)}, u32[]{:S(2)}, u32[]{:S(2)}) async-start(f32[16,16,128]{2,1,0:T(8,128)} %broadcast_in_dim.28), calls=%async_computation.2 | async-start | bytes 262144 | tf_op jit(solution)/shard_map/all_to_all | solution.py:25
  139.9 0.7 fusion.5
  140.6 3.5 %all-gather.6 = f32[128,1024]{1,0:T(8,128)S(1)} all-gather(f32[64,1024]{1,0:T(8,128)S(1)} %fusion.5), channel_id=8, replica_groups={{0,1},{3,2},{4,5},{7,6},{8,9},{11,10},{12,13},{15,14},{17,16},{18,19},{..., dimensions={0}, use_global_device_ids=true | all-gather | bytes 786432 | tf_op jit(solution)/shard_map/all_gather | solution.py:276
  144.1 0.3 reshape.64
  144.3 1.9 %copy.29 = f32[64,64,2,16]{1,3,2,0:T(8,128)} copy(f32[64,64,2,16]{0,3,1,2:T(8,128)S(1)} %bitcast.41) | data formatting | bytes 1048576 | tf_op jit(solution)/shard_map/transpose | solution.py:280
  146.2 0.6 broadcast_multiply_fusion
  146.8 4.6 %all-to-all-done.2 = f32[16,16,128]{2,1,0:T(8,128)S(1)} async-done(((f32[16,16,128]{2,1,0:T(8,128)}), f32[16,16,128]{2,1,0:T(8,128)S(1)}, u32[]{:S(2)}, u32[]{:S(2)}) %all-to-all-start.2) | async-done | bytes 131104 | tf_op jit(solution)/shard_map/all_to_all | solution.py:25
  151.5 8.6 %all-gather.5 = f32[64,128]{1,0:T(8,128)S(1)} all-gather(f32[16,128]{1,0:T(8,128)S(1)} %reduce_sum.39), channel_id=7, replica_groups={{0,1,2,3},{4,5,6,7},{8,9,10,11},{12,13,14,15},{16,17,18,19},{20,21,22,2..., dimensions={0}, use_global_device_ids=true | all-gather | bytes 40960 | tf_op jit(solution)/shard_map/all_gather | solution.py:269
  160.1 2.0 %shard_map.79 = f32[32,128]{1,0:T(8,128)} custom-call(f32[2,2,16,128]{3,2,1,0:T(8,128)S(1)} %bitcast.40), custom_call_target="tpu_custom_call" | custom-call | tf_op jit(solution)/shard_map/pallas_call | solution.py:62
  (14 shorter events, 0.1 us)
Async XLA Ops:
  0.6 0.9 copy-start
  0.6 0.8 copy-start.2
  0.7 0.9 copy-start.1
  135.9 15.5 %all-to-all-start.2 = ((f32[16,16,128]{2,1,0:T(8,128)}), f32[16,16,128]{2,1,0:T(8,128)S(1)}, u32[]{:S(2)}, u32[]{:S(2)}) async-start(f32[16,16,128]{2,1,0:T(8,128)} %broadcast_in_dim.28), calls=%async_computation.2 | async-start | bytes 262144 | tf_op jit(solution)/shard_map/all_to_all | solution.py:25

commit v11 on v10

--- a/solution.py
+++ b/solution.py
@@ -179,11 +179,6 @@
     lines_of_chips = [
         [row * depth + core_of(half, row, 0) for row in range(rows)] for half in range(depth)
     ]
-    teams = [
-        [col * depth + core_of(half, 0, col) for col in range(first, first + CLASSES)]
-        for first in range(0, cols, CLASSES)
-        for half in range(depth)
-    ]
     near = [
         list(range(first * depth, (first + half_team) * depth))
         for first in range(0, cols, half_team)
@@ -192,6 +187,18 @@
     for last in range(half_team - 1, cols, half_team):
         pair = [last, (last + 1) % cols]
         far.append(pair if last % CLASSES < half_team else pair[::-1])
+
+    def same_half(chosen):
+        return [
+            [col * depth + core_of(half, 0, col) for col in pair]
+            for pair in chosen
+            for half in range(depth)
+        ]
+
+    near_halves = same_half(
+        [list(range(first, first + half_team)) for first in range(0, cols, half_team)]
+    )
+    far_halves = same_half(far)
     slices = rank_three // (CLASSES * depth)
     flat = tensor.reshape(size_one * size_two, size_three)
 
@@ -237,8 +244,9 @@
         z_parts,
         got,
     )
-    projected = lax.all_gather(projected, ("cols", "depth"), axis_index_groups=teams)
-    projected = projected.reshape(-1, length_two)
+    for groups in (near_halves, far_halves):
+        projected = lax.all_gather(projected, ("cols", "depth"), axis_index_groups=groups)
+        projected = projected.reshape(-1, length_two)
     z_part = kernel_call(second_mode, (rank_two, length_two), projected, two_old)
     z_parts = lax.all_gather(z_part, "depth")
 

time: 162 us -> 164 us (1.012)
  blocking collectives: 138 us -> 140 us
    all_gather x1 -> x2, blocking collectives: 15.1 us -> 17.3 us  [body(): lax.all_gather(projected, ('cols', 'depth'), axis_index_groups=groups)]
where the time goes in v11:
time: 164 us
  blocking collectives  140 us (85%)
  Pallas kernels  8.15 us (5%)
  waiting for transfers between devices  4.64 us (3%)
  local copies, waits for them, and re-layouts  4.32 us (3%)
  starting transfers between devices  3.95 us (2%)
    all_to_all x1, blocking collectives, body(): lax.all_to_all(shard, EVERYWHERE, 0, 0, tiled=True, axis_index_groups=blo...  53.1 us
    all_gather x1, blocking collectives, body(): lax.all_gather(jnp.concatenate([own, one_packed], axis=0), ('rows', 'dept...  32.4 us
    all_gather x2, blocking collectives, body(): lax.all_gather(projected, ('cols', 'depth'), axis_index_groups=groups)  17.3 us
    all_to_all x1, blocking collectives, body(): lax.all_to_all(shard, 'cols', 0, 0, tiled=True)  9.54 us
    all_gather x1, blocking collectives, body(): z_parts = lax.all_gather(z_part, ('cols', 'depth'), axis_index_groups=near)  8.59 us
    pallas_call x5, Pallas kernels, kernel_call(): pl.pallas_call(kernel, out_shape=outs[0] if one else outs, in_specs=[whol...  8.15 us
    all_gather x1, blocking collectives, body(): lax.all_gather(z_part, ('cols', 'depth'), axis_index_groups=near)  6.07 us
    all_gather x1, blocking collectives, body(): z_parts = lax.all_gather(z_part, 'cols', axis_index_groups=far)  5.39 us
  transfers between devices with their start and end apart: 1, of which 1 were waited for; matrix products, arithmetic and copies ran while one was open for 2% of the time, Pallas kernels for 0%

profile of v11, /device:TPU:65, one launch (start us, length us, event | category | flops | bytes accessed | tf_op | source)
XLA Modules:
  0.0 163.6 jit_solution(5229171727889693335)
XLA Ops:
  0.6 0.0 copy-start
  0.6 0.0 copy-start.2
  0.7 0.0 copy-start.1
  0.7 0.8 fusion.2
  1.4 0.0 copy-done.2
  1.4 0.1 copy-done
  1.6 0.0 copy-done.1
  1.6 0.2 fusion.4
  1.8 0.1 pad_maximum_fusion.4
  1.9 0.1 pad_maximum_fusion.3
  2.0 53.1 %all_to_all.15 = f32[16,16,128]{2,1,0:T(8,128)S(1)} all-to-all(f32[16,16,128]{2,1,0:T(8,128)S(1)} %pad_maximum_fusion), channel_id=1, replica_groups={{0,1,3,2,4,5,7,6,8,9,11,10,12,13,15,14},{17,16,18,19,21,20,22,23,25,24,..., dimensions={0} | all-to-all | bytes 262144 | tf_op jit(solution)/shard_map/all_to_all | solution.py:218
  55.1 0.1 slice_bitcast_fusion.1
  55.2 0.1 copy.26
  55.3 0.1 reshape.58
  55.5 0.1 copy.25
  55.6 0.1 pad_maximum_fusion.1
  55.7 0.1 copy.27
  55.7 32.4 %all-gather = f32[1152,128]{1,0:T(8,128)S(1)} all-gather(f32[72,128]{1,0:T(8,128)S(1)} %copy.27), channel_id=2, replica_groups={{0,17,32,49,64,81,96,113,128,145,160,177,192,209,224,241},{1,16,33,48,6..., dimensions={0}, use_global_device_ids=true | all-gather | bytes 626688 | tf_op jit(solution)/shard_map/all_gather | solution.py:228
  88.2 1.5 shard_map.75
  89.6 6.1 %all-gather.1 = f32[256,256]{1,0:T(8,128)S(1)} all-gather(f32[64,256]{1,0:T(8,128)S(1)} %shard_map.75), channel_id=3, replica_groups={{0,1,2,3},{4,5,6,7},{8,9,10,11},{12,13,14,15},{16,17,18,19},{20,21,22,2..., dimensions={0}, use_global_device_ids=true | all-gather | bytes 327680 | tf_op jit(solution)/shard_map/all_gather | solution.py:238
  95.7 5.4 %all-gather.2 = f32[128,256]{1,0:T(8,128)S(1)} all-gather(f32[64,256]{1,0:T(8,128)S(1)} %reduce_sum.37), channel_id=4, replica_groups={{2,4},{8,6},{10,12},{0,14},{3,5},{9,7},{11,13},{1,15},{18,20},{24,22},{..., dimensions={0}, use_global_device_ids=true | all-gather | bytes 196608 | tf_op jit(solution)/shard_map/all_gather | solution.py:239
  101.1 1.8 %shard_map.76 = (f32[64,256]{1,0:T(8,128)S(1)}, f32[256,128]{1,0:T(8,128)S(1)}) custom-call(f32[2,64,256]{2,1,0:T(8,128)S(1)} %bitcast.38, f32[16,72,128]{2,1,0:T(8,128)S(1)} %bitcast.35), custom_call_target="tpu_custom_call" | custom-call | tf_op jit(solution)/shard_map/pallas_call | solution.py:62
  102.9 6.5 %all-gather.3 = f32[512,128]{1,0:T(8,128)S(1)} all-gather(f32[256,128]{1,0:T(8,128)S(1)} %get-tuple-element.31), channel_id=5, replica_groups={{0,3},{1,2},{4,7},{5,6},{8,11},{9,10},{12,15},{13,14},{16,19},{17,18},{..., dimensions={0}, use_global_device_ids=true | all-gather | bytes 393216 | tf_op jit(solution)/shard_map/all_gather | solution.py:248
  109.4 10.8 %all-gather.7.projected = f32[1024,128]{1,0:T(8,128)S(1)} all-gather(f32[512,128]{1,0:T(8,128)S(1)} %all-gather.3), channel_id=9, replica_groups={{3,4},{2,5},{8,7},{9,6},{11,12},{10,13},{0,15},{1,14},{19,20},{18,21},{..., dimensions={0}, use_global_device_ids=true | all-gather | bytes 786432 | tf_op jit(solution)/shard_map/all_gather | solution.py:248
  120.2 0.9 shard_map.77
  121.1 2.0 %all-gather.4 = f32[128,128]{1,0:T(8,128)S(1)} all-gather(f32[64,128]{1,0:T(8,128)S(1)} %shard_map.77), channel_id=6, replica_groups=mesh['groups'=2,'rows'=16,'cols'=8,'depth'=2] {'depth'}, dimensions={0}, use_global_device_ids=true | all-gather | bytes 98304 | tf_op jit(solution)/shard_map/all_gather | solution.py:251
  123.1 2.0 %shard_map.78 = (f32[64,128]{1,0:T(8,128)S(1)}, f32[16,64]{1,0:T(8,128)S(1)}, f32[16,64]{1,0:T(8,128)S(1)}, f32[256,16]{1,0:T(8,128)S(1)}) custom-call(f32[2,64,128]{2,1,0:T(8,128)S(1)} %bitcast.39, f32[1024,128]{1,0:T(8,128)S(1)} %all-gather.7.projected, f32[64,256]{1,0:T(8,128)S(1)} %get-tuple-element.32.one), custom_call_target="tpu_custom_call" | custom-call | tf_op jit(solution)/shard_map/pallas_call | solution.py:62
  125.1 0.1 all_gather_reshape.7
  125.2 1.9 %all_gather.59 = f32[2,16,256]{2,1,0:T(8,128)S(1)} all-gather(f32[1,16,256]{2,1,0:T(8,128)S(1)} %all_gather_reshape.7), channel_id=1, replica_groups={{0,1},{3,2},{4,5},{7,6},{8,9},{11,10},{12,13},{15,14},{17,16},{18,19},{..., dimensions={0}, use_global_device_ids=true | all-gather | bytes 49152 | tf_op jit(solution)/shard_map/all_gather | solution.py:266
  127.1 0.2 fusion
  127.3 9.5 %all_to_all.16 = f32[8,16,128]{2,1,0:T(8,128)S(1)} all-to-all(f32[8,16,128]{2,1,0:T(8,128)S(1)} %bitcast.48), channel_id=1, replica_groups=mesh['groups'=2,'rows'=16,'cols'=8,'depth'=2] {'cols'}, dimensions={0} | all-to-all | bytes 131072 | tf_op jit(solution)/shard_map/all_to_all | solution.py:273
  136.9 0.6 broadcast_in_dim.28
  137.5 4.0 %all-to-all-start.2 = ((f32[16,16,128]{2,1,0:T(8,128)}), f32[16,16,128]{2,1,0:T(8,128)S(1)}, u32[]{:S(2)}, u32[]{:S(2)}) async-start(f32[16,16,128]{2,1,0:T(8,128)} %broadcast_in_dim.28), calls=%async_computation.2 | async-start | bytes 262144 | tf_op jit(solution)/shard_map/all_to_all | solution.py:25
  141.5 0.7 fusion.5
  142.1 3.5 %all-gather.6 = f32[128,1024]{1,0:T(8,128)S(1)} all-gather(f32[64,1024]{1,0:T(8,128)S(1)} %fusion.5), channel_id=8, replica_groups={{0,1},{3,2},{4,5},{7,6},{8,9},{11,10},{12,13},{15,14},{17,16},{18,19},{..., dimensions={0}, use_global_device_ids=true | all-gather | bytes 786432 | tf_op jit(solution)/shard_map/all_gather | solution.py:284
  145.6 0.3 reshape.64
  145.9 1.9 %copy.29 = f32[64,64,2,16]{1,3,2,0:T(8,128)} copy(f32[64,64,2,16]{0,3,1,2:T(8,128)S(1)} %bitcast.41) | data formatting | bytes 1048576 | tf_op jit(solution)/shard_map/transpose | solution.py:288
  147.8 0.6 broadcast_multiply_fusion
  148.4 4.6 %all-to-all-done.2 = f32[16,16,128]{2,1,0:T(8,128)S(1)} async-done(((f32[16,16,128]{2,1,0:T(8,128)}), f32[16,16,128]{2,1,0:T(8,128)S(1)}, u32[]{:S(2)}, u32[]{:S(2)}) %all-to-all-start.2) | async-done | bytes 131104 | tf_op jit(solution)/shard_map/all_to_all | solution.py:25
  153.1 8.6 %all-gather.5 = f32[64,128]{1,0:T(8,128)S(1)} all-gather(f32[16,128]{1,0:T(8,128)S(1)} %reduce_sum.39), channel_id=7, replica_groups={{0,1,2,3},{4,5,6,7},{8,9,10,11},{12,13,14,15},{16,17,18,19},{20,21,22,2..., dimensions={0}, use_global_device_ids=true | all-gather | bytes 40960 | tf_op jit(solution)/shard_map/all_gather | solution.py:277
  161.6 2.0 %shard_map.79 = f32[32,128]{1,0:T(8,128)} custom-call(f32[2,2,16,128]{3,2,1,0:T(8,128)S(1)} %bitcast.40), custom_call_target="tpu_custom_call" | custom-call | tf_op jit(solution)/shard_map/pallas_call | solution.py:62
  (14 shorter events, 0.1 us)
Async XLA Ops:
  0.6 0.9 copy-start
  0.6 0.8 copy-start.2
  0.7 0.9 copy-start.1
  137.5 15.5 %all-to-all-start.2 = ((f32[16,16,128]{2,1,0:T(8,128)}), f32[16,16,128]{2,1,0:T(8,128)S(1)}, u32[]{:S(2)}, u32[]{:S(2)}) async-start(f32[16,16,128]{2,1,0:T(8,128)} %broadcast_in_dim.28), calls=%async_computation.2 | async-start | bytes 262144 | tf_op jit(solution)/shard_map/all_to_all | solution.py:25
